TPU v7x, 32 devices: a whole 2x2x4 slice. The times are simulated.
32 devices in a mesh: dp: 8 (over z, y), tensor: 4 (over x, core).
Axes of the slice: x: 2, y: 2, z: 4, core: 2. Of those that a mesh axis runs over, the one named last changes fastest.
Arguments:
- inputs: float32 [1024, 16, 512], P('tensor', 'dp'), may hold values from -6 to 6
- qkv_weight: bfloat16 [3, 512, 512], P(None, 'dp', 'tensor'), may hold values from -0.375 to 0.375
- out_weight: bfloat16 [512, 512], P('tensor', 'dp'), may hold values from -1 to 1
- up_weight: bfloat16 [512, 2048], P('dp', 'tensor'), may hold values from -0.25 to 0.25
- down_weight: bfloat16 [2048, 512], P('tensor', 'dp'), may hold values from -0.125 to 0.125
- gain_one: float32 [512], replicated, may hold values from 0.1 to 1.9
- shift_one: float32 [512], replicated, may hold values from -1.5 to 1.5
- gain_two: float32 [512], replicated, may hold values from 0.1 to 1.9
- shift_two: float32 [512], replicated, may hold values from -1.5 to 1.5
- lengths: int32 [16], P('dp'), may hold values from 512 to 1024, as said below
- teacher: float32 [1024, 16, 512], P('tensor', 'dp'), may hold values from -6 to 6
- cotangent: float32 [1024, 16, 512], P('tensor', 'dp'), may hold values from -6 to 6
Outputs:
- output: float32 [1024, 16, 512], P('tensor', 'dp')
- loss: float32 [], replicated
- grad_inputs: float32 [1024, 16, 512], P('tensor', 'dp')
- grad_qkv: float32 [3, 512, 512], P(None, 'dp', 'tensor')
- grad_out_weight: float32 [512, 512], P('tensor', 'dp')
- grad_up: float32 [512, 2048], P('dp', 'tensor')
- grad_down_weight: float32 [2048, 512], P('tensor', 'dp')
- grad_gain_one: float32 [512], replicated
- grad_shift_one: float32 [512], replicated
- grad_gain_two: float32 [512], replicated
- grad_shift_two: float32 [512], replicated
Inputs may be any that keep to these rules, and one draw needn't show every extreme that they name: `lengths`: some sequence has exactly 1024 valid tokens and some has exactly 512.
All inputs are finite; a program needn't handle non-finite values.
Results may differ from a plain program's by a relative error of at most 0.006.
The roundings to bfloat16 on the way count: a program that leaves them out, or rounds other values in their place, can miss the bound.
Values may be sent and summed in bfloat16 or wider, within the bound.
A program may use at most 128 MiB of HBM per device.

v0:
```python
from functools import partial
import math

import jax
import jax.numpy as jnp
from jax import lax
from jax.sharding import PartitionSpec as P

HD = 64


def norm_rows(values, gain, shift):
    center = values - jnp.mean(values, -1, keepdims=True)
    spread = jnp.mean(center * center, -1, keepdims=True)
    return center * lax.rsqrt(spread + 1e-05) * gain + shift


def angle_tables(positions, width):
    half = width // 2
    rates = jnp.exp(jnp.arange(half, dtype=jnp.float32) * (-2.0 * math.log(10000.0) / width))
    angles = positions.astype(jnp.float32)[:, None] * rates[None, :]
    cosine = jnp.concatenate([jnp.cos(angles), jnp.cos(angles)], -1)[:, None, None, :]
    sine = jnp.concatenate([jnp.sin(angles), jnp.sin(angles)], -1)[:, None, None, :]
    return (cosine, sine)


def turn_half(values):
    half = values.shape[-1] // 2
    return jnp.concatenate([-values[..., half:], values[..., :half]], -1)


def rotate(values, cosine, sine):
    return values * cosine + turn_half(values) * sine


def rotate_back(grads, cosine, sine):
    return grads * cosine - turn_half(grads * sine)


def shards(
    inputs,
    qkv_weight,
    out_weight,
    up_weight,
    down_weight,
    gain_one,
    shift_one,
    gain_two,
    shift_two,
    lengths,
    teacher,
    cotangent,
):
    tensor_size = lax.axis_size("tensor")
    own_rows, sequences, width = inputs.shape
    full_rows = own_rows * tensor_size
    local_width = qkv_weight.shape[2]
    local_heads = local_width // HD
    scale = HD ** (-0.5)
    block_rows = min(512, full_rows)
    starts = list(range(0, full_rows, block_rows))
    total = lax.psum(jnp.sum(lengths).astype(jnp.float32), "dp")
    positions = jnp.arange(full_rows)
    cosine, sine = angle_tables(positions, HD)
    own_positions = lax.axis_index("tensor") * own_rows + jnp.arange(own_rows)
    valid = (own_positions[:, None] < lengths[None, :]).astype(jnp.float32)[:, :, None]

    def allowed_for(start_row):
        query_pos = start_row + jnp.arange(block_rows)
        causal = positions[None, None, None, :] <= query_pos[None, None, :, None]
        return causal & (positions[None, None, None, :] < lengths[:, None, None, None])

    qkv_full, out_full = (
        lax.all_gather(qkv_weight, "dp", axis=1, tiled=True),
        lax.all_gather(out_weight, "dp", axis=1, tiled=True),
    )
    normed = norm_rows(inputs, gain_one, shift_one).astype(jnp.bfloat16)
    normed_all = lax.all_gather(normed, "tensor", axis=0, tiled=True)
    projected = jnp.einsum(
        "lsd,cdk->clsk", normed_all, qkv_full, preferred_element_type=jnp.float32
    )
    shaped = projected.reshape(3, full_rows, sequences, local_heads, HD)
    queries = rotate(shaped[0], cosine, sine).astype(jnp.bfloat16)
    keys_all = rotate(shaped[1], cosine, sine).astype(jnp.bfloat16)
    values_all = shaped[2].astype(jnp.bfloat16)

    def block_scores(start_row):
        block_queries = queries[start_row : start_row + block_rows]
        raw = jnp.einsum(
            "qshe,kshe->shqk", block_queries, keys_all, preferred_element_type=jnp.float32
        )
        return jnp.where(allowed_for(start_row), raw * scale, -1e30)

    mixed_blocks = []
    log_sums = []
    for start_row in starts:
        scores = block_scores(start_row)
        highest = jnp.max(scores, -1, keepdims=True)
        expd = jnp.exp(scores - highest)
        denom = jnp.sum(expd, -1, keepdims=True)
        probs = expd / denom
        log_sums.append(highest + jnp.log(denom))
        mixed_blocks.append(
            jnp.einsum(
                "shqk,kshe->qshe",
                probs.astype(jnp.bfloat16),
                values_all,
                preferred_element_type=jnp.float32,
            )
        )
    attended = (
        jnp.concatenate(mixed_blocks, 0)
        .reshape(full_rows, sequences, local_width)
        .astype(jnp.bfloat16)
    )
    slice_part = attended
    middle_state = inputs + lax.psum_scatter(
        jnp.einsum("lsk,kd->lsd", slice_part, out_full, preferred_element_type=jnp.float32),
        "tensor",
        scatter_dimension=0,
        tiled=True,
    )
    up_weight_gathered, down_weight_gathered = (
        lax.all_gather(up_weight, "dp", axis=0, tiled=True),
        lax.all_gather(down_weight, "dp", axis=1, tiled=True),
    )
    second_normed_rows = norm_rows(middle_state, gain_two, shift_two).astype(jnp.bfloat16)
    second_normed_gathered = lax.all_gather(second_normed_rows, "tensor", axis=0, tiled=True)
    activation_input = jnp.einsum(
        "agm,mt->agt",
        second_normed_gathered,
        up_weight_gathered,
        preferred_element_type=jnp.float32,
    )
    hidden_rows = jax.nn.gelu(activation_input, approximate=False).astype(jnp.bfloat16)
    slice_part = hidden_rows
    output = middle_state + lax.psum_scatter(
        jnp.einsum(
            "bzv,vc->bzc", slice_part, down_weight_gathered, preferred_element_type=jnp.float32
        ),
        "tensor",
        scatter_dimension=0,
        tiled=True,
    )
    differ = output - teacher
    square_part = jnp.sum(valid * differ * differ)
    factor = float(full_rows * sequences * lax.axis_size("dp")) / total
    seed = factor * valid * (cotangent + differ)
    unused_value, gelu_back = jax.vjp(partial(jax.nn.gelu, approximate=False), activation_input)
    grad_output_rows = lax.all_gather(seed.astype(jnp.bfloat16), "tensor", axis=0, tiled=True)
    grad_down_weight = jnp.einsum(
        "aoi,aop->ip", hidden_rows, grad_output_rows, preferred_element_type=jnp.float32
    )
    grad_hidden = jnp.einsum(
        "ecb,gb->ecg", grad_output_rows, down_weight_gathered, preferred_element_type=jnp.float32
    )
    grad_activation_input = gelu_back(grad_hidden)[0].astype(jnp.bfloat16)
    grad_up = jnp.einsum(
        "ckr,ckn->rn",
        second_normed_gathered,
        grad_activation_input,
        preferred_element_type=jnp.float32,
    )
    slice_part = grad_activation_input
    grad_normed_two = lax.psum_scatter(
        jnp.einsum(
            "bmq,eq->bme", slice_part, up_weight_gathered, preferred_element_type=jnp.float32
        ),
        "tensor",
        scatter_dimension=0,
        tiled=True,
    )
    unused_norm, norm_back_two = jax.vjp(norm_rows, middle_state, gain_two, shift_two)
    grad_middle_norm, grad_gain_two, grad_shift_two = norm_back_two(grad_normed_two)
    grad_middle = seed + grad_middle_norm
    grad_branch_rows = lax.all_gather(
        grad_middle.astype(jnp.bfloat16), "tensor", axis=0, tiled=True
    )
    grad_out_w = jnp.einsum(
        "lsk,lsd->kd", attended, grad_branch_rows, preferred_element_type=jnp.float32
    )
    grad_attended = jnp.einsum(
        "lsd,kd->lsk", grad_branch_rows, out_full, preferred_element_type=jnp.float32
    )
    grad_attended = grad_attended.astype(jnp.bfloat16).reshape(
        full_rows, sequences, local_heads, HD
    )
    grad_keys = jnp.zeros((full_rows, sequences, local_heads, HD), jnp.float32)
    grad_values = jnp.zeros((full_rows, sequences, local_heads, HD), jnp.float32)
    grad_query_blocks = []
    for block_index, start_row in enumerate(starts):
        scores = block_scores(start_row)
        probs = jnp.exp(scores - log_sums[block_index])
        block_grad = grad_attended[start_row : start_row + block_rows]
        grad_probs = jnp.einsum(
            "qshe,kshe->shqk", block_grad, values_all, preferred_element_type=jnp.float32
        )
        inner = jnp.sum(probs * grad_probs, -1, keepdims=True)
        grad_raw = (probs * (grad_probs - inner) * scale).astype(jnp.bfloat16)
        grad_query_blocks.append(
            jnp.einsum("shqk,kshe->qshe", grad_raw, keys_all, preferred_element_type=jnp.float32)
        )
        grad_keys = grad_keys + jnp.einsum(
            "shqk,qshe->kshe",
            grad_raw,
            queries[start_row : start_row + block_rows],
            preferred_element_type=jnp.float32,
        )
        grad_values = grad_values + jnp.einsum(
            "shqk,qshe->kshe",
            probs.astype(jnp.bfloat16),
            block_grad,
            preferred_element_type=jnp.float32,
        )
    grad_queries = jnp.concatenate(grad_query_blocks, 0)
    grad_projected = jnp.stack(
        [rotate_back(grad_queries, cosine, sine), rotate_back(grad_keys, cosine, sine), grad_values]
    )
    grad_projected = grad_projected.astype(jnp.bfloat16).reshape(
        3, full_rows, sequences, local_width
    )
    grad_qkv = jnp.einsum(
        "lsd,clsk->cdk", normed_all, grad_projected, preferred_element_type=jnp.float32
    )
    slice_part = grad_projected
    grad_normed = lax.psum_scatter(
        jnp.einsum("clsk,cdk->lsd", slice_part, qkv_full, preferred_element_type=jnp.float32),
        "tensor",
        scatter_dimension=0,
        tiled=True,
    )
    unused_first, norm_back_one = jax.vjp(norm_rows, inputs, gain_one, shift_one)
    grad_inputs_norm, grad_gain_one, grad_shift_one = norm_back_one(grad_normed)
    grad_inputs = grad_middle + grad_inputs_norm
    grad_qkv, grad_out_w, grad_up, grad_down_weight = (
        lax.psum_scatter(grad_qkv, "dp", scatter_dimension=1, tiled=True),
        lax.psum_scatter(grad_out_w, "dp", scatter_dimension=1, tiled=True),
        lax.psum_scatter(grad_up, "dp", scatter_dimension=0, tiled=True),
        lax.psum_scatter(grad_down_weight, "dp", scatter_dimension=1, tiled=True),
    )
    square_sum, grad_gain_one, grad_shift_one, grad_gain_two, grad_shift_two = lax.psum(
        (square_part, grad_gain_one, grad_shift_one, grad_gain_two, grad_shift_two),
        ("dp", "tensor"),
    )
    loss = square_sum / (total * width)
    return (
        output,
        loss,
        grad_inputs,
        grad_qkv,
        grad_out_w,
        grad_up,
        grad_down_weight,
        grad_gain_one,
        grad_shift_one,
        grad_gain_two,
        grad_shift_two,
    )


def solution(mesh):
    placed = (
        P("tensor", "dp", None),
        P(None, "dp", "tensor"),
        P("tensor", "dp"),
        P("dp", "tensor"),
        P("tensor", "dp"),
        P(),
        P(),
        P(),
        P(),
        P("dp"),
        P("tensor", "dp", None),
        P("tensor", "dp", None),
    )
    return jax.shard_map(
        shards,
        mesh=mesh,
        in_specs=placed,
        out_specs=(
            P("tensor", "dp", None),
            P(),
            P("tensor", "dp", None),
            P(None, "dp", "tensor"),
            P("tensor", "dp"),
            P("dp", "tensor"),
            P("tensor", "dp"),
            P(),
            P(),
            P(),
            P(),
        ),
        check_vma=False,
    )
```

profile of v0, /device:TPU:0, one launch (start us, length us, event | category | flops | bytes accessed | tf_op | source)
XLA Modules:
  0.0 849.3 jit_solution(6604862089245916614)
XLA Ops:
  13.0 32.3 %all_gather.26 = bf16[128,512]{0,1:T(8,128)(2,1)S(1)} all-gather(bf16[128,64]{0,1:T(8,128)(2,1)S(1)} %copy-done.47), channel_id=1, replica_groups=mesh['dp'=8,'tensor'=4] {'dp'}, dimensions={1}, use_global_device_ids=true | all-gather | bytes 147456 | tf_op jit(solution)/shard_map/all_gather | solution.py:75
  46.8 31.5 %all_gather.25 = bf16[3,512,128]{2,1,0:T(8,128)(2,1)S(1)} all-gather(bf16[3,64,128]{2,1,0:T(8,128)(2,1)S(1)} %copy-done.35), channel_id=1, replica_groups=mesh['dp'=8,'tensor'=4] {'dp'}, dimensions={1}, use_global_device_ids=true | all-gather | bytes 442368 | tf_op jit(solution)/shard_map/all_gather | solution.py:74
  88.8 4.7 fusion.4
  103.2 45.8 %reduce-scatter.8.cloned.1.call-done = f32[256,2,512]{2,0,1:T(8,128)} async-done(((f32[1024,2,512]{2,0,1:T(8,128)}), f32[256,2,512]{2,0,1:T(8,128)}) %reduce-scatter.8.cloned.1.call-update) | async-done | bytes 1048592 | tf_op jit(solution)/shard_map/reduce_scatter | solution.py:117
  152.0 31.5 %all_gather.28 = bf16[512,512]{1,0:T(8,128)(2,1)S(1)} all-gather(bf16[64,512]{1,0:T(8,128)(2,1)S(1)} %copy-done.34), channel_id=1, replica_groups=mesh['dp'=8,'tensor'=4] {'dp'}, dimensions={0}, use_global_device_ids=true | all-gather | bytes 589824 | tf_op jit(solution)/shard_map/all_gather | solution.py:124
  183.4 31.6 %all_gather.29 = bf16[512,512]{0,1:T(8,128)(2,1)S(1)} all-gather(bf16[512,64]{0,1:T(8,128)(2,1)} %param.16), channel_id=1, replica_groups=mesh['dp'=8,'tensor'=4] {'dp'}, dimensions={1}, use_global_device_ids=true | all-gather | bytes 589824 | tf_op jit(solution)/shard_map/all_gather | solution.py:125
  215.0 4.5 fusion.108
  219.5 10.7 %multiply_convert_fusion.2 = (bf16[1024,2,512]{2,0,1:T(8,128)(2,1)S(1)}, f32[1024,2,512]{2,0,1:T(8,128)}) fusion(f32[1024,2,512]{2,0,1:T(8,128)S(1)} %get-tuple-element.113, u8[1024,512]{1,0:T(8,128)(4,1)S(1)} %get-tuple-element.67, u8[1024,512]{1,0:T(8,128)(4,1)S(1)} %get-tuple-element.66), kind=kLoop, calls=%fused_computation.38 | loop fusion | flops 73400320 | bytes 11534336 | tf_op jit(solution)/shard_map/convert_element_type | solution.py:135
  236.3 22.0 %psum.43 = f32[]{:T(128)} all-reduce(f32[]{:T(128)S(6)} %convert_element_type.90), channel_id=1, replica_groups=mesh['dp'=8,'tensor'=4] {'dp'}, use_global_device_ids=true, to_apply=%region_13.14 | all-reduce | flops 1 | bytes 8 | tf_op jit(solution)/shard_map/psum | solution.py:62
  259.6 20.2 %reduce-scatter.10.cloned.1.call-done = f32[256,2,512]{2,0,1:T(8,128)} async-done(((f32[1024,2,512]{2,0,1:T(8,128)}), f32[256,2,512]{2,0,1:T(8,128)}) %reduce-scatter.10.cloned.1.call-update) | async-done | bytes 1048592 | tf_op jit(solution)/shard_map/reduce_scatter | solution.py:137
  279.8 3.5 fusion.164
  283.4 22.7 %all-gather.9.cloned.1.call-done = bf16[1024,2,512]{2,0,1:T(8,128)(2,1)} async-done(((bf16[256,2,512]{2,0,1:T(8,128)(2,1)}), bf16[1024,2,512]{2,0,1:T(8,128)(2,1)}) %all-gather.9.cloned.1.call-update) | async-done | bytes 2097168 | tf_op jit(solution)/shard_map/all_gather | solution.py:150
  306.1 6.7 add_convert_fusion
  317.4 44.7 %reduce-scatter.12.cloned.1.call-done = f32[256,2,512]{2,0,1:T(8,128)} async-done(((f32[1024,2,512]{2,0,1:T(8,128)}), f32[256,2,512]{2,0,1:T(8,128)}) %reduce-scatter.12.cloned.1.call-update) | async-done | bytes 1048592 | tf_op jit(solution)/shard_map/reduce_scatter | solution.py:165
  372.5 19.0 %all-gather.11.cloned.1.call-done = bf16[1024,2,512]{2,0,1:T(8,128)(2,1)} async-done(((bf16[256,2,512]{2,0,1:T(8,128)(2,1)}), bf16[1024,2,512]{2,0,1:T(8,128)(2,1)}) %all-gather.11.cloned.1.call-update) | async-done | bytes 2097168 | tf_op jit(solution)/shard_map/all_gather | solution.py:176
  395.3 4.5 fusion.172
  399.9 23.4 %fusion.17 = f32[2,2,64,512]{3,2,1,0:T(8,128)} fusion(bf16[1024,2,2,64]{0,3,2,1:T(8,128)(2,1)S(1)} %copy-done.33, f32[2,2,512,1024]{3,2,1,0:T(8,128)} %fusion.172, f32[2,2,512,1024]{3,2,1,0:T(8,128)} %copy-done.6, f32[2,2,512]{2,1,0:T(2,128)S(1)} %copy-done.49, pred[2,512,1024]{2,1,0:T(8,128)(4,1)} %copy-done.16), kind=kOutput, calls=%fused_computation.23 | convolution fusion | flops 291507200 | bytes 18882560 | tf_op jit(solution)/shard_map/shqk,kshe->qshe/dot_general | solution.py:201
  423.3 19.2 %fusion.14 = f32[2,2,64,1024]{3,2,1,0:T(8,128)} fusion(f32[2,2,512,1024]{3,2,1,0:T(8,128)} %fusion.172, f32[2,2,512,1024]{3,2,1,0:T(8,128)} %copy-done.6, f32[2,2,512]{2,1,0:T(2,128)S(1)} %copy-done.49, pred[2,512,1024]{2,1,0:T(8,128)(4,1)} %copy-done.16, bf16[1024,2,2,64]{0,3,2,1:T(8,128)(2,1)} %copy-done.31), kind=kOutput, calls=%fused_computation.22 | convolution fusion | flops 291507200 | bytes 36978688 | tf_op jit(solution)/shard_map/shqk,qshe->kshe/dot_general | solution.py:203
  442.5 4.5 fusion.173
  447.0 5.0 fusion.56
  452.1 3.5 fusion.91
  458.6 18.7 %fusion.24 = f32[2,2,64,512]{3,2,1,0:T(8,128)} fusion(bf16[1024,2,2,64]{0,3,2,1:T(8,128)(2,1)} %copy-done.32, f32[2,2,512,1024]{3,2,1,0:T(8,128)} %fusion.173, f32[2,2,512,1024]{3,2,1,0:T(8,128)} %copy-done.5, f32[2,2,512]{2,1,0:T(2,128)S(1)} %copy-done.48, pred[2,512,1024]{2,1,0:T(8,128)(4,1)} %copy-done.14), kind=kOutput, calls=%fused_computation.26 | convolution fusion | flops 291507200 | bytes 18882560 | tf_op jit(solution)/shard_map/shqk,kshe->qshe/dot_general | solution.py:201
  477.2 20.5 %maximum_multiply_fusion.3 = (f32[1024,2,2,64]{0,3,2,1:T(8,128)}, f32[1024,2,2,64]{0,3,2,1:T(8,128)}, f32[1024,2,2,64]{0,3,2,1:T(8,128)}) fusion(f32[512,2,2,64]{0,3,2,1:T(8,128)} %bitcast.122, f32[512,2,2,64]{0,3,2,1:T(8,128)S(1)} %bitcast.121, f32[1024,64]{0,1:T(8,128)S(1)} %copy-done.25, f32[2,2,64,1024]{3,2,1,0:T(8,128)} %fusion.14, ...), kind=kOutput, calls=%fused_computation.107 | convolution fusion | flops 292555776 | bytes 41435136 | tf_op jit(solution)/shard_map/shqk,qshe->kshe/dot_general | solution.py:203
  516.0 4.6 convolution_bitcast_fusion
  520.6 4.7 convolution_bitcast_fusion.2
  525.6 4.5 convolution_bitcast_fusion.1
  537.9 56.4 %all-reduce.4.cloned.1.call-done = f32[3,512,128]{2,0,1:T(4,128)} async-done(((f32[3,512,128]{2,0,1:T(4,128)}), f32[3,512,128]{2,0,1:T(4,128)}) %all-reduce.4.cloned.1.call-update) | async-done | bytes 786448
  595.9 45.1 %reduce-scatter.14.cloned.1.call-done = f32[256,2,512]{2,0,1:T(8,128)} async-done(((f32[1024,2,512]{2,0,1:T(8,128)}), f32[256,2,512]{2,0,1:T(8,128)}) %reduce-scatter.14.cloned.1.call-update) | async-done | bytes 1048592 | tf_op jit(solution)/shard_map/reduce_scatter | solution.py:226
  644.7 40.0 %all-reduce.1 = (f32[]{:T(128)}, f32[512]{0:T(512)}, f32[512]{0:T(512)}, f32[512]{0:T(512)}, f32[512]{0:T(512)}) all-reduce(f32[]{:T(128)} %fusion.98, f32[512]{0:T(512)S(1)} %get-tuple-element.68, f32[512]{0:T(512)S(1)} %get-tuple-element.73, f32[512]{0:T(512)S(1)} %copy-done.50, ...), channel_id=1, replica_groups=mesh['dp'=8,'tensor'=4] {'dp','tensor'}, use_global_device_ids=true, to_apply=%region_11.12 | all-reduce | flops 2049 | bytes 16392 | tf_op jit(solution)/shard_map/psum | solution.py:241
  688.9 20.3 %reduce-scatter.18.cloned.1.call-done = f32[64,512]{1,0:T(8,128)} async-done(((f32[512,512]{1,0:T(8,128)}), f32[64,512]{1,0:T(8,128)}) %reduce-scatter.18.cloned.1.call-update) | async-done | bytes 131088 | tf_op jit(solution)/shard_map/reduce_scatter | solution.py:238
  709.2 67.1 %reduce-scatter.20.cloned.1.call-done = f32[512,64]{0,1:T(8,128)} async-done(((f32[512,512]{0,1:T(8,128)}), f32[512,64]{0,1:T(8,128)}) %reduce-scatter.20.cloned.1.call-update) | async-done | bytes 131088 | tf_op jit(solution)/shard_map/reduce_scatter | solution.py:239
  776.4 64.8 %reduce-scatter.16.cloned.1.call-done = f32[128,64]{0,1:T(8,128)} async-done(((f32[128,512]{0,1:T(8,128)}), f32[128,64]{0,1:T(8,128)}) %reduce-scatter.16.cloned.1.call-update) | async-done | bytes 32784 | tf_op jit(solution)/shard_map/reduce_scatter | solution.py:237
  (223 shorter events, 91.6 us)
Async XLA Ops:
  7.2 39.6 %copy-start.35 = (bf16[3,64,128]{2,1,0:T(8,128)(2,1)S(1)}, bf16[3,64,128]{2,1,0:T(8,128)(2,1)}, u32[]{:S(2)}) copy-start(bf16[3,64,128]{2,1,0:T(8,128)(2,1)} %param.13) | copy-start | bytes 147460
  7.2 71.1 %copy-start.52 = (s32[2]{0:T(128)S(1)}, s32[2]{0:T(128)}, u32[]{:S(2)}) copy-start(s32[2]{0:T(128)} %param.21) | copy-start | bytes 28
  7.2 72.5 %all-gather.5.cloned.1.call-start = ((), (), s32[]{:S(2)}) async-start(), calls=%async_computation.7 | async-start | bytes 2621440 | tf_op jit(solution)/shard_map/all_gather | solution.py:78
  10.5 72.6 %copy-start.43 = (f32[256,2]{0,1:T(2,128)}, f32[256,2]{0,1:T(2,128)S(1)}, u32[]{:S(2)}) copy-start(f32[256,2]{0,1:T(2,128)S(1)} %multiply_reduce_fusion.7) | copy-start | bytes 6148
  10.5 72.6 %copy-start.39 = (f32[256,2]{0,1:T(2,128)}, f32[256,2]{0,1:T(2,128)S(1)}, u32[]{:S(2)}) copy-start(f32[256,2]{0,1:T(2,128)S(1)} %fusion.130) | copy-start | bytes 6148
  12.9 136.1 %reduce-scatter.8.cloned.1.call-start = ((), (), s32[]{:S(2)}) async-start(), calls=%async_computation.8 | async-start | bytes 5242880 | tf_op jit(solution)/shard_map/reduce_scatter | solution.py:117
  79.7 16.9 %copy-start.16 = (pred[2,512,1024]{2,1,0:T(8,128)(4,1)}, pred[2,512,1024]{2,1,0:T(8,128)(4,1)S(1)}, u32[]{:S(2)}) copy-start(pred[2,512,1024]{2,1,0:T(8,128)(4,1)S(1)} %get-tuple-element.107) | copy-start | bytes 3145732
  100.5 48.5 %copy-start = (f32[256,2,512]{2,1,0:T(2,128)S(1)}, f32[256,2,512]{2,1,0:T(2,128)}, u32[]{:S(2)}) copy-start(f32[256,2,512]{2,1,0:T(2,128)} %param.12) | copy-start | bytes 3145732
  103.2 47.7 %copy-start.46 = (f32[512]{0:T(512)S(1)}, f32[512]{0:T(512)}, u32[]{:S(2)}) copy-start(f32[512]{0:T(512)} %param.19) | copy-start | bytes 6148
  103.2 47.7 %copy-start.57 = (f32[512]{0:T(512)S(1)}, f32[512]{0:T(512)}, u32[]{:S(2)}) copy-start(f32[512]{0:T(512)} %param.20) | copy-start | bytes 6148
  103.2 48.8 %copy-start.34 = (bf16[64,512]{1,0:T(8,128)(2,1)S(1)}, bf16[64,512]{1,0:T(8,128)(2,1)}, u32[]{:S(2)}) copy-start(bf16[64,512]{1,0:T(8,128)(2,1)} %param.15) | copy-start | bytes 196612
  103.2 111.8 %all-gather.7.cloned.1.call-start = ((), (), s32[]{:S(2)}) async-start(), calls=%async_computation.9 | async-start | bytes 2621440 | tf_op jit(solution)/shard_map/all_gather | solution.py:128
  151.9 127.9 %reduce-scatter.10.cloned.1.call-start = ((), (), s32[]{:S(2)}) async-start(), calls=%async_computation.10 | async-start | bytes 5242880 | tf_op jit(solution)/shard_map/reduce_scatter | solution.py:137
  183.4 36.1 %copy-start.21 = (bf16[512,512]{1,0:T(8,128)(2,1)}, bf16[512,512]{1,0:T(8,128)(2,1)S(1)}, u32[]{:S(2)}) copy-start(bf16[512,512]{1,0:T(8,128)(2,1)S(1)} %all_gather.28) | copy-start | bytes 1572868
  234.9 71.2 %all-gather.9.cloned.1.call-start = ((), (), s32[]{:S(2)}) async-start(), calls=%async_computation.11 | async-start | bytes 2621440 | tf_op jit(solution)/shard_map/all_gather | solution.py:150
  283.3 78.7 %reduce-scatter.12.cloned.1.call-start = ((), (), s32[]{:S(2)}) async-start(), calls=%async_computation.12 | async-start | bytes 5242880 | tf_op jit(solution)/shard_map/reduce_scatter | solution.py:165
  317.4 74.1 %all-gather.11.cloned.1.call-start = ((), (), s32[]{:S(2)}) async-start(), calls=%async_computation.13 | async-start | bytes 2621440 | tf_op jit(solution)/shard_map/all_gather | solution.py:176
  367.8 27.6 %copy-start.11 = (bf16[1,1024,2,128]{1,3,0,2:T(8,128)(2,1)S(1)}, bf16[1,1024,2,128]{1,3,0,2:T(8,128)(2,1)}, u32[]{:S(2)}) copy-start(bf16[1,1024,2,128]{1,3,0,2:T(8,128)(2,1)} %copy-done.10) | copy-start | bytes 1572868
  368.7 225.6 %all-reduce.4.cloned.1.call-start = ((), (), s32[]{:S(2)}) async-start(), calls=%async_computation.18 | async-start | bytes 2097152
  423.3 19.2 %copy-start.28 = (bf16[512,2,128]{0,2,1:T(8,128)(2,1)S(1)}, bf16[512,2,128]{0,2,1:T(8,128)(2,1)}, u32[]{:S(2)}) copy-start(bf16[512,2,128]{0,2,1:T(8,128)(2,1)} %get-tuple-element.100) | copy-start | bytes 786436
  458.6 18.7 %copy-start.25 = (f32[1024,64]{0,1:T(8,128)S(1)}, f32[1024,64]{0,1:T(8,128)}, u32[]{:S(2)}) copy-start(f32[1024,64]{0,1:T(8,128)} %pad_maximum_fusion.6) | copy-start | bytes 786436
  515.9 125.2 %reduce-scatter.14.cloned.1.call-start = ((), (), s32[]{:S(2)}) async-start(), calls=%async_computation.14 | async-start | bytes 5242880 | tf_op jit(solution)/shard_map/reduce_scatter | solution.py:226
  520.6 188.6 %reduce-scatter.18.cloned.1.call-start = ((), (), s32[]{:S(2)}) async-start(), calls=%async_computation.16 | async-start | bytes 1179648 | tf_op jit(solution)/shard_map/reduce_scatter | solution.py:238
  525.4 251.0 %reduce-scatter.20.cloned.1.call-start = ((), (), s32[]{:S(2)}) async-start(), calls=%async_computation.17 | async-start | bytes 1179648 | tf_op jit(solution)/shard_map/reduce_scatter | solution.py:239
  530.1 110.9 %copy-start.41 = (f32[512]{0:T(512)S(1)}, f32[512]{0:T(512)}, u32[]{:S(2)}) copy-start(f32[512]{0:T(512)} %param.17) | copy-start | bytes 6148
  530.2 311.0 %reduce-scatter.16.cloned.1.call-start = ((), (), s32[]{:S(2)}) async-start(), calls=%async_computation.15 | async-start | bytes 294912 | tf_op jit(solution)/shard_map/reduce_scatter | solution.py:237
  534.0 108.8 %copy-start.44 = (f32[256,2]{0,1:T(2,128)S(1)}, f32[256,2]{0,1:T(2,128)}, u32[]{:S(2)}) copy-start(f32[256,2]{0,1:T(2,128)} %copy-done.43) | copy-start | bytes 6148
  534.0 108.8 %copy-start.40 = (f32[256,2]{0,1:T(2,128)S(1)}, f32[256,2]{0,1:T(2,128)}, u32[]{:S(2)}) copy-start(f32[256,2]{0,1:T(2,128)} %copy-done.39) | copy-start | bytes 6148
  536.2 108.5 %copy-start.50 = (f32[512]{0:T(512)S(1)}, f32[512]{0:T(512)}, u32[]{:S(2)}) copy-start(f32[512]{0:T(512)} %get-tuple-element.70) | copy-start | bytes 6148
  536.3 108.5 %copy-start.51 = (f32[512]{0:T(512)S(1)}, f32[512]{0:T(512)}, u32[]{:S(2)}) copy-start(f32[512]{0:T(512)} %get-tuple-element.72) | copy-start | bytes 6148
  536.3 148.5 %copy-start.2 = (f32[256,2,512]{2,0,1:T(8,128)S(1)}, f32[256,2,512]{2,0,1:T(8,128)}, u32[]{:S(2)}) copy-start(f32[256,2,512]{2,0,1:T(8,128)} %get-tuple-element.83) | copy-start | bytes 3145732
  641.1 43.7 %copy-start.3 = (f32[256,2,512]{2,0,1:T(8,128)S(1)}, f32[256,2,512]{2,0,1:T(8,128)}, u32[]{:S(2)}) copy-start(f32[256,2,512]{2,0,1:T(8,128)} %reduce-scatter.14.cloned.1.call-done) | copy-start | bytes 3145732
  (41 other events, 205.1 us)
Sparse Core Ops, SparseCore 0:
  13.0 25.2 all-gather.4
  103.3 45.6 reduce-scatter.7
  152.0 22.5 all-gather.6
  235.0 44.7 reduce-scatter.9
  283.5 22.5 all-gather.8
  317.5 44.5 reduce-scatter.11
  368.9 22.5 all-gather.10
  516.0 78.2 all-reduce.3
  596.9 44.1 reduce-scatter.13
  644.9 64.2 reduce-scatter.17
  713.2 63.1 reduce-scatter.19
  780.1 60.9 reduce-scatter.15
where the time goes:
time: 853 us; the launch traced here: 849 us
  waiting for transfers between devices  406 us (48%)
  blocking collectives  189 us (22%)
  matrix products  154 us (18%)
  other arithmetic  55.5 us (7%)
  local copies, waits for them, and re-layouts  24.8 us (3%)
  between operations  19.7 us (2%)
    reduce_scatter x1, waiting for transfers between devices, shards(): lax.psum_scatter(grad_down_weight, 'dp', scatter_dimension=1, tiled=True)  67.1 us
    reduce_scatter x1, waiting for transfers between devices, shards(): lax.psum_scatter(grad_out_w, 'dp', scatter_dimension=1, tiled=True)  64.8 us
    unnamed x13, waiting for transfers between devices  56.6 us
    reduce_scatter x1, waiting for transfers between devices, shards(): lax.psum_scatter(jnp.einsum('lsk,kd->lsd', slice_part, out_full, preferre...  45.8 us
    reduce_scatter x1, waiting for transfers between devices, shards(): lax.psum_scatter(jnp.einsum('clsk,cdk->lsd', slice_part, qkv_full, prefer...  45.1 us
    reduce_scatter x1, waiting for transfers between devices, shards(): lax.psum_scatter(jnp.einsum('bmq,eq->bme', slice_part, up_weight_gathered...  44.7 us
    dot_general x2, matrix products, shards(): jnp.einsum('shqk,kshe->qshe', grad_raw, keys_all, preferred_element_type=...  42.1 us
    psum x1, blocking collectives, shards(): lax.psum((square_part, grad_gain_one, grad_shift_one, grad_gain_two, grad...  40 us
  transfers between devices with their start and end apart: 12, of which 10 were waited for; matrix products, arithmetic and copies ran while one was open for 4% of the time, Pallas kernels for 0%

commit v1 on v0

v1 whole, which is shorter than its diff:
```python
import math

import jax
import jax.numpy as jnp
import numpy as np
from jax import lax
from jax.experimental import pallas as pl
from jax.experimental.pallas import tpu as pltpu
from jax.sharding import PartitionSpec as P

HD = 64
F32 = jnp.float32
BF16 = jnp.bfloat16
MESH = pl.DeviceIdType.MESH
VMEM_LIMIT = 60 * 1024 * 1024

NN = (((1,), (0,)), ((), ()))
NT = (((1,), (1,)), ((), ()))


def dot(a, b, dims=NN):
    return lax.dot_general(a, b, dims, preferred_element_type=F32)


class Place:
    def __init__(self, sizes):
        dp, tensor = lax.axis_index("dp"), lax.axis_index("tensor")
        self.sizes = sizes
        self.at = {"z": dp // sizes["y"], "y": dp % sizes["y"], "x": tensor // 2, "c": tensor % 2}

    def moved(self, axis, delta):
        size = self.sizes[axis]
        if size == 2:
            return 1 - self.at[axis]
        return lax.rem(self.at[axis] + (delta % size), size)

    def device(self, **moves):
        at = dict(self.at)
        for axis, delta in moves.items():
            at[axis] = self.moved(axis, delta)
        return (at["z"] * self.sizes["y"] + at["y"], at["x"] * 2 + at["c"])

    def peers(self):
        out = [self.device(x=1), self.device(c=1), self.device(x=1, c=1), self.device(y=1)]
        out += [self.device(z=delta) for delta in range(1, self.sizes["z"])]
        return out

    def meet(self):
        barrier = pltpu.get_barrier_semaphore()
        peers = self.peers()
        for peer in peers:
            pl.semaphore_signal(barrier, inc=1, device_id=peer, device_id_type=MESH)
        return lambda: pl.semaphore_wait(barrier, len(peers))


def remote(src, dst, send, recv, device):
    return pltpu.make_async_remote_copy(
        src_ref=src, dst_ref=dst, send_sem=send, recv_sem=recv, device_id=device, device_id_type=MESH
    )


class Gather:
    def __init__(self, place, view, order, send, recv, base):
        self.place, self.view, self.order = place, view, order
        self.send, self.recv, self.base = send, recv, base
        self.have = {}
        self.open = []
        self.sent = []

    @staticmethod
    def count(sizes, order):
        return sum(sizes[axis] - 1 for axis in order)

    def part(self, **changed):
        where = dict(self.place.at)
        where.update(self.have)
        where.update(changed)
        return self.view(where)

    def start(self):
        axis = self.order[0]
        size = self.place.sizes[axis]
        mine = self.part()
        self.open = []
        for delta in range(1, size):
            slot = self.base
            self.base += 1
            copy = remote(mine, mine, self.send.at[slot], self.recv.at[slot], self.place.device(**{axis: delta}))
            copy.start()
            theirs = self.part(**{axis: self.place.moved(axis, -delta)})
            self.open.append(
                remote(theirs, theirs, self.send.at[slot], self.recv.at[slot], self.place.device(**{axis: delta}))
            )
            self.sent.append(copy)

    def arrive(self):
        for copy in self.open:
            copy.wait_recv()
        self.open = []
        self.have[self.order[0]] = slice(None)
        self.order = self.order[1:]

    def finish(self):
        for copy in self.sent:
            copy.wait_send()
        self.sent = []


def lanes(shape, limit):
    return lax.broadcasted_iota(jnp.int32, shape, 1) < limit


def token_rows(ref, seq, rows):
    return [ref[pl.ds(2 * j + seq, rows, stride=8), :] for j in range(4)]


def row_mean(parts):
    total = parts[0]
    for part in parts[1:]:
        total = total + part
    return jnp.sum(total, -1, keepdims=True) * (1.0 / (128 * len(parts)))


def normalize(parts):
    mean = row_mean(parts)
    center = [part - mean for part in parts]
    spread = row_mean([part * part for part in center])
    scale = lax.rsqrt(spread + 1e-05)
    return center, scale


def rope(value, cos, sin_a, sin_b):
    return value * cos + pltpu.roll(value, 96, 1) * sin_a + pltpu.roll(value, 32, 1) * sin_b


def rope_back(grad, cos, sin_a, sin_b):
    return grad * cos - pltpu.roll(grad, 96, 1) * sin_a - pltpu.roll(grad, 32, 1) * sin_b


def rope_tables(rows):
    half = HD // 2
    rates = np.exp(np.arange(half, dtype=np.float32) * np.float32(-2.0 * math.log(10000.0) / HD))
    angles = np.arange(rows, dtype=np.float32)[:, None] * rates.astype(np.float32)[None, :]
    cos, sin, zero = np.cos(angles), np.sin(angles), np.zeros_like(angles)
    tables = [[cos] * 4, [-sin, zero] * 2, [zero, sin] * 2]
    return jnp.asarray(np.stack([np.concatenate(table, -1) for table in tables]).astype(np.float32))


def front_kernel(
    sizes,
    rows,
    block,
    lengths,
    x_ref,
    qkv_shard,
    out_shard,
    up_shard,
    down_shard,
    gain,
    shift,
    tables,
    ff_all,
    out_all,
    qkv_all,
    counts,
    normed_all,
    q_all,
    k_all,
    v_all,
    lse,
    attended,
    own_normed,
    own_attended,
    local_sem,
    send,
    recv,
    send2,
    recv2,
):
    place = Place(sizes)
    at = place.at
    x, c, z, y = at["x"], at["c"], at["z"], at["y"]
    own = rows // 4
    met = place.meet()

    def ff_view(w):
        return ff_all.at[w["x"], w["c"], w["z"], w["y"]]

    def local(index, src, dst):
        copy = pltpu.make_async_copy(src, dst, local_sem.at[index])
        copy.start()
        return copy

    def x_lane(index):
        return pl.ds(pl.multiple_of(index * 128, 128), 128)

    def out_at(w):
        lane = slice(None) if isinstance(w["x"], slice) else x_lane(w["x"])
        return out_all.at[w["c"], w["z"], w["y"], :, lane]

    def qkv_at(w):
        lane = slice(None) if isinstance(w["x"], slice) else x_lane(w["x"])
        return qkv_all.at[:, w["z"], w["y"], :, lane]

    copies = [
        local(0, qkv_shard, qkv_at(at)),
        local(1, out_shard, out_at(at)),
        local(2, up_shard, ff_all.at[x, c, z, y, :, pl.ds(0, 512)]),
        local(3, down_shard, ff_all.at[x, c, z, y, :, pl.ds(512, 512)]),
    ]
    total = lengths[0]
    for s in range(1, 2):
        total = total + lengths[s]
    counts[z, y] = jnp.full((8, 128), total.astype(F32))

    base = 0
    plans = []
    for view, order in (
        (qkv_at, "zyx"),
        (out_at, "zyxc"),
        (ff_view, "zyxc"),
        (lambda w: counts.at[w["z"], w["y"]], "zy"),
    ):
        plans.append(Gather(place, view, order, send, recv, base))
        base += Gather.count(sizes, order)
    qkv_g, out_g, ff_g, count_g = plans

    for s in range(2):
        center, scale = normalize(token_rows(x_ref, s, own))
        for j in range(4):
            lane = pl.ds(128 * j, 128)
            value = center[j] * scale * gain[:, lane] + shift[:, lane]
            own_normed[s, :, lane] = value.astype(BF16)
    for copy in copies:
        copy.wait()
    met()
    mine = pl.ds(pl.multiple_of((x * 2 + c) * own, own), own)
    keep = local(0, own_normed.at[x], normed_all.at[mine])
    tokens = []
    for index, (seq, moves) in enumerate(((1 - x, {"x": 1}), (1 - x, {"x": 1, "c": 1}), (x, {"c": 1}))):
        copy = remote(own_normed.at[seq], normed_all.at[mine], send2.at[index], recv2.at[index], place.device(**moves))
        copy.start()
        who = dict(at)
        for axis in moves:
            who[axis] = 1 - at[axis]
        theirs = normed_all.at[pl.ds(pl.multiple_of((who["x"] * 2 + who["c"]) * own, own), own)]
        tokens.append((copy, remote(theirs, theirs, send2.at[index], recv2.at[index], place.device(**moves))))
    qkv_g.start()
    count_g.start()
    qkv_g.arrive()
    qkv_g.start()
    count_g.arrive()
    count_g.start()
    qkv_g.arrive()
    qkv_g.start()
    out_g.start()
    ff_g.start()
    keep.wait()
    for sent, came in tokens:
        came.wait_recv()
    qkv_g.arrive()

    w_qkv = [qkv_all[i].reshape(-1, 256) for i in range(3)]

    def project(index, carry):
        here = pl.ds(pl.multiple_of(index * block, block), block)
        normed = normed_all[here, :]
        cos, sin_a, sin_b = (tables[i, here, :] for i in range(3))
        for i, ref in ((0, q_all), (1, k_all), (2, v_all)):
            value = dot(normed, w_qkv[i])
            for pair in range(2):
                lane = pl.ds(128 * pair, 128)
                part = value[:, 128 * pair : 128 * pair + 128]
                if i < 2:
                    part = rope(part, cos, sin_a, sin_b)
                if i == 0:
                    part = part.astype(BF16) * jnp.asarray(HD**-0.5, BF16)
                ref[here, lane] = part.astype(BF16)
        return carry

    lax.fori_loop(0, rows // block, project, 0)
    count_g.arrive()
    out_g.arrive()
    out_g.start()
    ff_g.arrive()
    ff_g.start()

    length = lengths[x]
    half = lanes((block, 128), HD)
    zero = jnp.zeros((block, 128), BF16)

    def attend(pair, carry):
        lane = pl.ds(pl.multiple_of(pair * 128, 128), 128)
        for qb in range(rows // block):
            here = pl.ds(qb * block, block)
            keys = (qb + 1) * block
            queries = q_all[here, lane]
            k_part = k_all[pl.ds(0, keys), lane]
            v_part = v_all[pl.ds(0, keys), lane]
            key_pos = lax.broadcasted_iota(jnp.int32, (block, keys), 1)
            query_pos = lax.broadcasted_iota(jnp.int32, (block, keys), 0) + qb * block
            allowed = key_pos <= query_pos
            if keys > rows // 2:
                allowed = allowed & (key_pos < length)
            mixed = []
            for head in range(2):
                masked = jnp.where(half, queries, zero) if head == 0 else jnp.where(half, zero, queries)
                scores = jnp.where(allowed, dot(masked, k_part, NT), -1e30)
                highest = jnp.max(scores, -1, keepdims=True)
                expd = jnp.exp(scores - highest)
                denom = jnp.sum(expd, -1, keepdims=True)
                probs = (expd * (1.0 / denom)).astype(BF16)
                mixed.append(dot(probs, v_part))
                wide = jnp.broadcast_to(highest + jnp.log(denom), (block, 128))
                lse[pair * 2 + head, :, here] = jnp.transpose(wide)[:8]
            own_attended[here, lane] = jnp.where(half, mixed[0], mixed[1]).astype(BF16)
        return carry

    lax.fori_loop(0, 2, attend, 0)
    out_g.arrive()
    out_g.start()
    ff_g.arrive()
    ff_g.start()

    def rows_of(tx, tc):
        return pl.ds(pl.multiple_of((tx * 2 + tc) * own, own), own)

    keep2 = local(1, own_attended.at[rows_of(x, c)], attended.at[c, x])
    moved = []
    for index, moves in enumerate(({"x": 1}, {"x": 1, "c": 1}, {"c": 1})):
        to = dict(at)
        for axis in moves:
            to[axis] = 1 - at[axis]
        copy = remote(
            own_attended.at[rows_of(to["x"], to["c"])],
            attended.at[c, x],
            send2.at[3 + index],
            recv2.at[3 + index],
            place.device(**moves),
        )
        copy.start()
        theirs = attended.at[to["c"], to["x"]]
        moved.append((copy, remote(theirs, theirs, send2.at[3 + index], recv2.at[3 + index], place.device(**moves))))
    out_g.arrive()
    out_g.start()
    ff_g.arrive()
    ff_g.start()
    keep2.wait()
    for sent, came in moved:
        came.wait_recv()
    out_g.arrive()
    ff_g.arrive()
    for plan in plans:
        plan.finish()
    for sent, came in tokens + moved:
        sent.wait_send()


def front(sizes, rows, lengths, x, qkv, out, up, down, gain, shift, tables):
    zs, ys = sizes["z"], sizes["y"]
    shard = qkv.shape[1]
    own = rows // 4
    block = 256
    orders = ("zyx", "zyxc", "zyxc", "zy")
    slots = sum(Gather.count(sizes, order) for order in orders)
    any_spec = pl.BlockSpec(memory_space=pl.ANY)
    vmem = pl.BlockSpec(memory_space=pltpu.VMEM)
    shapes = [
        ((2, 2, zs, ys, shard, 1024), BF16),
        ((2, zs, ys, shard, 256), BF16),
        ((3, zs, ys, shard, 256), BF16),
        ((zs, ys, 8, 128), F32),
        ((rows, 512), BF16),
        ((rows, 256), BF16),
        ((rows, 256), BF16),
        ((rows, 256), BF16),
        ((4, 8, rows), F32),
        ((2, 2, own, 256), BF16),
    ]
    return pl.pallas_call(
        lambda *refs: front_kernel(sizes, rows, block, *refs),
        out_shape=[jax.ShapeDtypeStruct(*shape) for shape in shapes],
        in_specs=[pl.BlockSpec(memory_space=pltpu.SMEM), vmem] + [any_spec] * 4 + [vmem] * 3,
        out_specs=[vmem] * len(shapes),
        scratch_shapes=[
            pltpu.VMEM((2, own, 512), BF16),
            pltpu.VMEM((rows, 256), BF16),
            pltpu.SemaphoreType.DMA((4,)),
            pltpu.SemaphoreType.DMA((slots,)),
            pltpu.SemaphoreType.DMA((slots,)),
            pltpu.SemaphoreType.DMA((6,)),
            pltpu.SemaphoreType.DMA((6,)),
        ],
        name="front",
        compiler_params=pltpu.CompilerParams(
            collective_id=0, has_side_effects=True, vmem_limit_bytes=VMEM_LIMIT
        ),
    )(lengths, x, qkv, out, up, down, gain, shift, tables)


def gelu_parts(value):
    cdf = 0.5 + 0.5 * lax.erf(value * (2.0**-0.5))
    density = jnp.exp(-0.5 * value * value) * ((2.0 * math.pi) ** -0.5)
    return value * cdf, cdf + value * density


def middle_kernel(
    own,
    tensor_total,
    lengths,
    counts,
    x_ref,
    teacher,
    cotangent,
    attended,
    ff_all,
    out_all,
    gain,
    shift,
    output,
    grad_middle,
    grad_attended,
    grad_ff,
    grad_out,
    stats,
    middle,
    seed,
    slope,
    hidden,
    total_sum,
):
    tokens = 2 * own
    tensor = lax.axis_index("tensor")
    count = jnp.sum(counts[...], axis=0)[0:1]
    factor = tensor_total / count
    valid = []
    for s in range(2):
        rows = pl.ds(s * own, own)
        attn = dot(attended[0, s], out_all[0], NT) + dot(attended[1, s], out_all[1], NT)
        parts = token_rows(x_ref, s, own)
        for j in range(4):
            middle[rows, pl.ds(128 * j, 128)] = parts[j] + attn[:, 128 * j : 128 * j + 128]
        position = tensor * own + lax.broadcasted_iota(jnp.int32, (own, 128), 0)
        valid.append((position < lengths[s]).astype(F32))
    value = middle[...]
    mean = jnp.mean(value, -1, keepdims=True)
    center = value - mean
    scale = lax.rsqrt(jnp.mean(center * center, -1, keepdims=True) + 1e-05)
    normed = (center * scale * gain[...] + shift[...]).astype(BF16)
    normed_t = jnp.transpose(normed)

    total_sum[...] = jnp.zeros_like(total_sum)

    def up(t, carry):
        before = dot(normed, ff_all[t, :, pl.ds(0, 512)])
        act, slope_t = gelu_parts(before)
        act = act.astype(BF16)
        slope[t] = slope_t
        hidden[t] = act
        total_sum[...] += dot(act, ff_all[t, :, pl.ds(512, 512)], NT)
        return carry

    lax.fori_loop(0, 4, up, 0)

    square = jnp.zeros((own, 128), F32)
    for s in range(2):
        rows = pl.ds(s * own, own)
        want = token_rows(teacher, s, own)
        weight = token_rows(cotangent, s, own)
        for j in range(4):
            lane = pl.ds(128 * j, 128)
            out = middle[rows, lane] + total_sum[rows, lane]
            output[pl.ds(2 * j + s, own, stride=8), :] = out
            differ = out - want[j]
            square = square + valid[s] * differ * differ
            seed[rows, lane] = factor * valid[s] * (weight[j] + differ)
    grad_f = seed[...].astype(BF16)
    grad_f_t = jnp.transpose(grad_f)
    total_sum[...] = jnp.zeros_like(total_sum)

    def down(t, carry):
        grad_hidden = dot(grad_f, ff_all[t, :, pl.ds(512, 512)])
        grad_before = (slope[t] * grad_hidden).astype(BF16)
        grad_ff[t, :, pl.ds(0, 512)] = dot(normed_t, grad_before).astype(BF16)
        grad_ff[t, :, pl.ds(512, 512)] = dot(grad_f_t, hidden[t]).astype(BF16)
        total_sum[...] += dot(grad_before, ff_all[t, :, pl.ds(0, 512)], NT)
        return carry

    lax.fori_loop(0, 4, down, 0)

    grad_normed = total_sum[...]
    unit = (middle[...] - mean) * scale
    stats[...] = jnp.zeros_like(stats)
    stats[0:1, 0:128] = jnp.sum(square, 0, keepdims=True)
    stats[8:9] = jnp.sum(grad_normed * unit, 0, keepdims=True)
    stats[16:17] = jnp.sum(grad_normed, 0, keepdims=True)
    scaled = grad_normed * gain[...]
    inner = jnp.mean(scaled * unit, -1, keepdims=True)
    grad = seed[...] + scale * (scaled - jnp.mean(scaled, -1, keepdims=True) - unit * inner)
    grad_middle[...] = grad
    branch = grad.astype(BF16)
    branch_t = jnp.transpose(branch)
    for k in range(2):
        grad_out[k] = (dot(branch_t[:, :own], attended[k, 0]) + dot(branch_t[:, own:], attended[k, 1])).astype(BF16)
        back = dot(branch, out_all[k]).astype(BF16)
        for s in range(2):
            grad_attended[k, s] = back[s * own : s * own + own]


def middle_part(own, tensor_total, lengths, counts, x, teacher, cotangent, attended, ff_all, out_all, gain, shift):
    tokens = 2 * own
    vmem = pl.BlockSpec(memory_space=pltpu.VMEM)
    shapes = [
        (x.shape, F32),
        ((tokens, 512), F32),
        ((2, 2, own, 256), BF16),
        ((4, 512, 1024), BF16),
        ((2, 512, 256), BF16),
        ((24, 512), F32),
    ]
    return pl.pallas_call(
        lambda *refs: middle_kernel(own, tensor_total, *refs),
        out_shape=[jax.ShapeDtypeStruct(*shape) for shape in shapes],
        in_specs=[pl.BlockSpec(memory_space=pltpu.SMEM)] + [vmem] * 9,
        out_specs=[vmem] * len(shapes),
        scratch_shapes=[
            pltpu.VMEM((tokens, 512), F32),
            pltpu.VMEM((tokens, 512), F32),
            pltpu.VMEM((4, tokens, 512), F32),
            pltpu.VMEM((4, tokens, 512), BF16),
            pltpu.VMEM((tokens, 512), F32),
        ],
        name="middle",
        compiler_params=pltpu.CompilerParams(vmem_limit_bytes=VMEM_LIMIT),
    )(lengths, counts, x, teacher, cotangent, attended, ff_all, out_all, gain, shift)


class Scatter:
    def __init__(self, place, view, order, landing, send, recv, base):
        self.place, self.view, self.order, self.landing = place, view, order, landing
        self.send, self.recv, self.base = send, recv, base
        self.left = list(order)
        self.where = dict(place.at)
        for axis in order:
            self.where[axis] = slice(None)
        self.open = []
        self.sent = []

    def part(self, view=None, **changed):
        where = dict(self.where)
        where.update(changed)
        return (view or self.view)(where)

    def start(self):
        axis = self.left[0]
        phase = len(self.order) - len(self.left)
        self.open = []
        for delta in range(1, self.place.sizes[axis]):
            slot = self.base
            self.base += 1
            source = self.part(**{axis: self.place.moved(axis, delta)})
            copy = remote(
                source,
                self.landing[phase].at[delta - 1],
                self.send.at[slot],
                self.recv.at[slot],
                self.place.device(**{axis: delta}),
            )
            copy.start()
            self.open.append(copy)
            self.sent.append(copy)

    def arrive(self, final=None):
        axis = self.left[0]
        phase = len(self.order) - len(self.left)
        for copy in self.open:
            copy.wait_recv()
        count = len(self.open)
        self.open = []
        self.where[axis] = self.place.at[axis]
        self.left = self.left[1:]
        rest = [a for a in "xczy" if a in self.left and not (a == "x" and self.lane_x)]
        sizes = [self.place.sizes[a] for a in rest]
        landing = self.landing[phase]

        def add(index, carry):
            chosen = {}
            for a, size in zip(reversed(rest), reversed(sizes)):
                chosen[a] = lax.rem(index, size)
                index = index // size
            mine = self.part(**chosen)
            total = mine[...].astype(F32)
            kept = self.part(view=self.work, **chosen) if self.work else mine
            for i in range(count):
                piece = landing.at[i]
                total = total + self.piece(piece, chosen, rest)[...].astype(F32)
            if final is None:
                kept[...] = total.astype(BF16)
            else:
                final[...] = total
            return carry

        steps = math.prod(sizes)
        if steps == 1:
            add(0, 0)
        else:
            lax.fori_loop(0, steps, add, 0)
        if self.work:
            self.view, self.work = self.work, None

    lane_x = False
    lead = 0
    work = None

    def piece(self, landing, chosen, rest):
        index = (slice(None),) * self.lead + tuple(chosen[a] for a in rest)
        return landing.at[index] if index else landing

    def finish(self):
        for copy in self.sent:
            copy.wait_send()


def landing_shapes(sizes, order, dims, tail, lead=(), lane_x=0):
    left = list(order)
    shapes = []
    for axis in order:
        left.remove(axis)
        shape = (sizes[axis] - 1,) + lead + tuple(sizes[a] for a in dims if a in left)
        wide = tail[1]
        if lane_x:
            wide = lane_x * (2 if "x" in left else 1)
        shapes.append(shape + (tail[0], wide))
    return shapes


UP_ORDER, DOWN_ORDER, OUT_ORDER, QKV_ORDER = "cxyz", "cyxz", "cxyz", "xyz"


def back_kernel(
    sizes,
    rows,
    block,
    lengths,
    grad_attended,
    q_all,
    k_all,
    v_all,
    lse,
    normed_all,
    qkv_all,
    grad_middle,
    x_ref,
    gain,
    tables,
    grad_ff,
    grad_out,
    stats,
    grad_inputs,
    up_final,
    down_final,
    out_final,
    qkv_final,
    stats_final,
    g_all,
    k_t,
    grad_q,
    grad_k,
    grad_v,
    grad_proj,
    grad_qkv,
    grad_n,
    ff_work,
    out_work,
    from_core,
    to_x,
    from_x,
    stat_send,
    stat_land,
    local_sem,
    send,
    recv,
    send2,
    recv2,
    *landing,
):
    place = Place(sizes)
    at = place.at
    x, c, z, y = at["x"], at["c"], at["z"], at["y"]
    own = rows // 4
    met = place.meet()

    def mine(tx, tc):
        return pl.ds(pl.multiple_of((tx * 2 + tc) * own, own), own)

    def x_lane(index):
        if isinstance(index, slice):
            return index
        return pl.ds(pl.multiple_of(index * 128, 128), 128)

    def half_view(start):
        return lambda w: grad_ff.at[w["x"], w["c"], w["z"], w["y"], :, pl.ds(start, 512)]

    def out_view(w):
        return grad_out.at[w["c"], w["z"], w["y"], :, x_lane(w["x"])]

    def qkv_view(w):
        return grad_qkv.at[:, w["z"], w["y"], :, x_lane(w["x"])]

    base = 0
    plans = []
    used = 0
    for view, order, lead, lane_x in (
        (half_view(0), UP_ORDER, 0, False),
        (half_view(512), DOWN_ORDER, 0, False),
        (out_view, OUT_ORDER, 0, True),
        (qkv_view, QKV_ORDER, 1, True),
    ):
        plan = Scatter(place, view, order, landing[used : used + len(order)], send, recv, base)
        plan.lead, plan.lane_x = lead, lane_x
        plans.append(plan)
        used += len(order)
        base += sum(sizes[axis] - 1 for axis in order)
    up_s, down_s, out_s, qkv_s = plans
    up_s.work = lambda w: ff_work.at[w["x"], w["z"], w["y"], :, pl.ds(0, 512)]
    down_s.work = lambda w: ff_work.at[w["x"], w["z"], w["y"], :, pl.ds(512, 512)]
    out_s.work = lambda w: out_work.at[w["z"], w["y"], :, x_lane(w["x"])]

    met()
    keep = pltpu.make_async_copy(grad_attended.at[c, x], g_all.at[mine(x, c)], local_sem.at[0])
    keep.start()
    moved = []
    for index, moves in enumerate(({"x": 1}, {"x": 1, "c": 1}, {"c": 1})):
        to = dict(at)
        for axis in moves:
            to[axis] = 1 - at[axis]
        copy = remote(
            grad_attended.at[to["c"], to["x"]],
            g_all.at[mine(x, c)],
            send2.at[index],
            recv2.at[index],
            place.device(**moves),
        )
        copy.start()
        theirs = g_all.at[mine(to["x"], to["c"])]
        moved.append((copy, remote(theirs, theirs, send2.at[index], recv2.at[index], place.device(**moves))))
    for plan in (up_s, down_s, out_s):
        plan.start()
    for pair in range(2):
        k_t[pair] = jnp.transpose(k_all[:, pl.ds(128 * pair, 128)])
    normed_t = jnp.transpose(normed_all[...])
    keep.wait()
    for sent, came in moved:
        came.wait_recv()

    length = lengths[x]
    half = lanes((block, 128), HD)
    zero = jnp.zeros((block, 128), BF16)
    upper = lax.broadcasted_iota(jnp.int32, (128, block), 0) < HD

    def attend(pair, blocks):
        lane = pl.ds(128 * pair, 128)
        for qb in blocks:
            here = pl.ds(qb * block, block)
            keys = (qb + 1) * block
            seen = pl.ds(0, keys)
            queries = q_all[here, lane]
            grads = g_all[here, lane]
            k_part = k_all[seen, lane]
            v_part = v_all[seen, lane]
            key_pos = lax.broadcasted_iota(jnp.int32, (keys, block), 0)
            query_pos = lax.broadcasted_iota(jnp.int32, (keys, block), 1) + qb * block
            allowed = key_pos <= query_pos
            if keys > rows // 2:
                allowed = allowed & (key_pos < length)
            dq = []
            for head in range(2):
                if head == 0:
                    q_m, g_m = jnp.where(half, queries, zero), jnp.where(half, grads, zero)
                else:
                    q_m, g_m = jnp.where(half, zero, queries), jnp.where(half, zero, grads)
                scores = dot(k_part, q_m, NT)
                probs = jnp.where(allowed, jnp.exp(scores - lse[pair * 2 + head, 0:1, here]), 0.0)
                grad_probs = dot(v_part, g_m, NT)
                inner = jnp.sum(probs * grad_probs, 0, keepdims=True)
                grad_raw = (probs * (grad_probs - inner)).astype(BF16)
                add_k = dot(grad_raw, q_m)
                add_v = dot(probs.astype(BF16), g_m)
                if qb == rows // block - 1 and head == 0:
                    grad_k[seen, lane] = add_k
                    grad_v[seen, lane] = add_v
                else:
                    grad_k[seen, lane] += add_k
                    grad_v[seen, lane] += add_v
                dq.append(dot(k_t[pair, :, seen], grad_raw))
            grad_q[here, lane] = jnp.transpose(jnp.where(upper, dq[0], dq[1])) * HD**-0.5

    last = rows // block - 1
    attend(0, [last])
    for plan in (up_s, down_s, out_s):
        plan.arrive()
        plan.start()
    attend(0, range(last - 1, -1, -1))
    attend(1, [last])
    for plan in (out_s, up_s, down_s):
        plan.arrive()
        plan.start()
    attend(1, range(last - 1, -1, -1))

    def turned(index, carry):
        here = pl.ds(pl.multiple_of(index * block, block), block)
        cos, sin_a, sin_b = (tables[i, here, :] for i in range(3))
        total = jnp.zeros((block, 512), F32)
        for i, ref in ((0, grad_q), (1, grad_k), (2, grad_v)):
            for pair in range(2):
                lane = pl.ds(128 * pair, 128)
                part = ref[here, lane]
                if i < 2:
                    part = rope_back(part, cos, sin_a, sin_b)
                grad_proj[i, here, lane] = part.astype(BF16)
            total = total + dot(grad_proj[i, here, :], qkv_all[i], NT)
        grad_n[here, :] = total
        return carry

    lax.fori_loop(0, rows // block, turned, 0)
    core = []
    for i in range(2):
        copy = remote(
            grad_n.at[mine(i, 1 - c)], from_core.at[i], send2.at[3 + i], recv2.at[3 + i], place.device(c=1)
        )
        copy.start()
        core.append(copy)
    deep = sizes["z"] * sizes["y"]
    shard = 512 // deep
    for i in range(3):
        value = dot(normed_t, grad_proj[i]).astype(BF16)
        grad_qkv[i] = value.reshape(sizes["z"], sizes["y"], shard, 256)
    for copy in core:
        copy.wait_recv()
    to_x[...] = (grad_n[mine(1 - x, c), :] + from_core[1 - x]).astype(BF16)
    cross = remote(to_x, from_x, send2.at[5], recv2.at[5], place.device(x=1))
    cross.start()
    qkv_s.start()
    for plan in (out_s, up_s, down_s):
        plan.arrive()
        plan.start()
    stat_send[0] = jnp.zeros_like(stat_send[0])
    stat_send[0, 0:24] = stats[...]
    cross.wait_recv()
    grad_gain = [jnp.zeros((1, 128), F32)] * 4
    grad_shift = [jnp.zeros((1, 128), F32)] * 4
    for s in range(2):
        center, scale = normalize(token_rows(x_ref, s, own))
        local = grad_n[mine(x, c), :] + from_core[x]
        far = from_x[...].astype(F32)
        chosen = jnp.where(x == s, local, far)
        grads = [chosen[:, 128 * j : 128 * j + 128] for j in range(4)]
        units = [part * scale for part in center]
        scaled = [grads[j] * gain[:, pl.ds(128 * j, 128)] for j in range(4)]
        mean = row_mean(scaled)
        inner = row_mean([scaled[j] * units[j] for j in range(4)])
        for j in range(4):
            part = grad_middle[pl.ds(s * own, own), pl.ds(128 * j, 128)]
            grad_inputs[pl.ds(2 * j + s, own, stride=8), :] = part + scale * (scaled[j] - mean - units[j] * inner)
            grad_gain[j] = grad_gain[j] + jnp.sum(grads[j] * units[j], 0, keepdims=True)
            grad_shift[j] = grad_shift[j] + jnp.sum(grads[j], 0, keepdims=True)
    for j in range(4):
        stat_send[0, 24:25, 128 * j : 128 * j + 128] = grad_gain[j]
        stat_send[0, 32:33, 128 * j : 128 * j + 128] = grad_shift[j]

    slot = 6
    landed = 0
    stat_sent = []
    for phase, axis in enumerate("cxyz"):
        came = []
        for delta in range(1, sizes[axis]):
            copy = remote(
                stat_send.at[phase], stat_land.at[landed], send2.at[slot], recv2.at[slot], place.device(**{axis: delta})
            )
            copy.start()
            came.append((copy, landed))
            stat_sent.append(copy)
            slot += 1
            landed += 1
        if phase < 3:
            qkv_s.arrive(None if phase < 2 else qkv_final)
            if phase < 2:
                qkv_s.start()
        if phase == 1:
            out_s.arrive(out_final)
            up_s.arrive(up_final)
            down_s.arrive(down_final)
        total = stat_send[phase]
        for copy, index in came:
            copy.wait_recv()
            total = total + stat_land[index]
        if phase < 3:
            stat_send[phase + 1] = total
        else:
            stats_final[...] = total
    for plan in plans:
        plan.finish()
    for copy in [sent for sent, _ in moved] + core + [cross] + stat_sent:
        copy.wait_send()


def back(sizes, rows, lengths, grad_attended, q, k, v, lse, normed, qkv, grad_middle, x, gain, tables, grad_ff, grad_out, stats):
    zs, ys = sizes["z"], sizes["y"]
    shard = 512 // (zs * ys)
    own = rows // 4
    block = 256
    vmem = pl.BlockSpec(memory_space=pltpu.VMEM)
    shapes = [x.shape, (shard, 512), (shard, 512), (shard, 128), (3, shard, 128), (40, 512)]
    lands = landing_shapes(sizes, UP_ORDER, "xczy", (shard, 512))
    lands += landing_shapes(sizes, DOWN_ORDER, "xczy", (shard, 512))
    lands += landing_shapes(sizes, OUT_ORDER, "czy", (shard, 256), lane_x=128)
    lands += landing_shapes(sizes, QKV_ORDER, "zy", (shard, 256), lead=(3,), lane_x=128)
    slots = sum(shape[0] for shape in lands)
    meets = sum(sizes[axis] - 1 for axis in "cxyz")
    return pl.pallas_call(
        lambda *refs: back_kernel(sizes, rows, block, *refs),
        out_shape=[jax.ShapeDtypeStruct(shape, F32) for shape in shapes],
        in_specs=[pl.BlockSpec(memory_space=pltpu.SMEM)] + [vmem] * 14,
        out_specs=[vmem] * len(shapes),
        scratch_shapes=[
            pltpu.VMEM((rows, 256), BF16),
            pltpu.VMEM((2, 128, rows), BF16),
            pltpu.VMEM((rows, 256), F32),
            pltpu.VMEM((rows, 256), F32),
            pltpu.VMEM((rows, 256), F32),
            pltpu.VMEM((3, rows, 256), BF16),
            pltpu.VMEM((3, zs, ys, shard, 256), BF16),
            pltpu.VMEM((rows, 512), F32),
            pltpu.VMEM((2, zs, ys, shard, 1024), BF16),
            pltpu.VMEM((zs, ys, shard, 256), BF16),
            pltpu.VMEM((2, own, 512), F32),
            pltpu.VMEM((own, 512), BF16),
            pltpu.VMEM((own, 512), BF16),
            pltpu.VMEM((4, 40, 512), F32),
            pltpu.VMEM((meets, 40, 512), F32),
            pltpu.SemaphoreType.DMA((1,)),
            pltpu.SemaphoreType.DMA((slots,)),
            pltpu.SemaphoreType.DMA((slots,)),
            pltpu.SemaphoreType.DMA((6 + meets,)),
            pltpu.SemaphoreType.DMA((6 + meets,)),
        ]
        + [pltpu.VMEM(shape, BF16) for shape in lands],
        name="back",
        compiler_params=pltpu.CompilerParams(
            collective_id=1, has_side_effects=True, vmem_limit_bytes=VMEM_LIMIT
        ),
    )(lengths, grad_attended, q, k, v, lse, normed, qkv, grad_middle, x, gain, tables, grad_ff, grad_out, stats)


def solution(mesh):
    dp, tensor = mesh.shape["dp"], mesh.shape["tensor"]
    sizes = {"z": dp // 2, "y": 2, "x": tensor // 2, "c": 2}

    def shards(
        inputs, qkv_weight, out_weight, up_weight, down_weight, gain_one, shift_one, gain_two, shift_two, lengths,
        teacher, cotangent,
    ):
        own, sequences, width = inputs.shape
        rows = own * tensor
        shard = width // dp

        def packed(value):
            view = value.reshape(own, sequences, width // 128, 128).transpose(0, 2, 1, 3)
            return view.reshape(own * sequences * (width // 128), 128)

        def unpacked(value):
            view = value.reshape(own, width // 128, sequences, 128).transpose(0, 2, 1, 3)
            return view.reshape(own, sequences, width)

        x = packed(inputs)
        tables = rope_tables(rows)
        ff_all, out_all, qkv_all, counts, normed, q, k, v, lse, attended = front(
            sizes, rows, lengths, x, qkv_weight, out_weight.T, up_weight, down_weight.T, gain_one[None],
            shift_one[None], tables,
        )
        output, grad_middle, grad_attended, grad_ff, grad_out, stats = middle_part(
            own, float(rows * sequences * dp), lengths, counts.reshape(dp, 8, 128), x, packed(teacher),
            packed(cotangent), attended, ff_all.reshape(tensor, width, 1024), out_all.reshape(2, width, 256),
            gain_two[None], shift_two[None],
        )
        grad_inputs, up, down, out, qkv, sums = back(
            sizes, rows, lengths, grad_attended, q, k, v, lse, normed, qkv_all.reshape(3, width, 256), grad_middle, x,
            gain_one[None], tables, grad_ff.reshape(ff_all.shape), grad_out.reshape(out_all.shape), stats,
        )
        total = jnp.sum(counts[:, :, 0, 0])
        loss = jnp.sum(sums[0, :128]) / (total * width)
        return (
            unpacked(output), loss, unpacked(grad_inputs), qkv, out.T, up, down.T, sums[24], sums[32], sums[8], sums[16],
        )

    tokens, rows_dp, cols_dp = P("tensor", "dp", None), P("dp", "tensor"), P("tensor", "dp")
    heads = P(None, "dp", "tensor")
    return jax.shard_map(
        shards,
        mesh=mesh,
        in_specs=(tokens, heads, cols_dp, rows_dp, cols_dp, P(), P(), P(), P(), P("dp"), tokens, tokens),
        out_specs=(tokens, P(), tokens, heads, cols_dp, rows_dp, cols_dp, P(), P(), P(), P()),
        check_vma=False,
    )
```

time: 853 us -> 188 us (0.22)
  waiting for transfers between devices: 406 us -> 0 us
  blocking collectives: 189 us -> 0 us
  Pallas kernels: 0 us -> 171 us
  matrix products: 154 us -> 0 us
  other arithmetic: 55.5 us -> 2.65 us
  between operations: 19.7 us -> 3.1 us
  local copies, waits for them, and re-layouts: 24.8 us -> 9.96 us
    reduce_scatter x7 -> x0, waiting for transfers between devices: 308 us -> none  [the longest x1 67.1 us: shards(): lax.psum_scatter(grad_down_weight, 'dp', scatter_dimension=1, tiled=True)]
    pallas_call x0 -> x3, Pallas kernels: none -> 171 us  [the longest x1 77.5 us: back(): pl.pallas_call(lambda *refs: back_kernel(sizes, rows, block, *refs), out_...]
    dot_general x24 -> x0, matrix products: 154 us -> none  [the longest x2 42.1 us: shards(): jnp.einsum('shqk,kshe->qshe', grad_raw, keys_all, preferred_element_type=...]
    all_gather x4 -> x0, blocking collectives: 127 us -> none  [the longest x1 32.3 us: shards(): lax.all_gather(out_weight, 'dp', axis=1, tiled=True)]
    psum x2 -> x0, blocking collectives: 62 us -> none  [the longest x1 40 us: shards(): lax.psum((square_part, grad_gain_one, grad_shift_one, grad_gain_two, grad...]
    unnamed x13 -> x0, waiting for transfers between devices: 56.6 us -> none
    all_gather x4 -> x0, waiting for transfers between devices: 41.7 us -> none  [the longest x1 22.7 us: shards(): lax.all_gather(seed.astype(jnp.bfloat16), 'tensor', axis=0, tiled=True)]
    convert_element_type x8 -> x0, other arithmetic: 19.2 us -> none  [the longest x1 10.7 us: shards(): jax.nn.gelu(activation_input, approximate=False).astype(jnp.bfloat16)]
  transfers between devices with their start and end apart: 12 -> 0, of which waited for: 10 -> 0; matrix products, arithmetic and copies ran while one was open for 4% -> 0% of each run, Pallas kernels for 0% -> 0%
where the time goes in v1:
time: 188 us; the launch traced here: 187 us
  Pallas kernels  171 us (91%)
  local copies, waits for them, and re-layouts  9.96 us (5%)
  between operations  3.1 us (2%)
  other arithmetic  2.65 us (1%)
    pallas_call x1, Pallas kernels, back(): pl.pallas_call(lambda *refs: back_kernel(sizes, rows, block, *refs), out_...  77.5 us
    pallas_call x1, Pallas kernels, front(): pl.pallas_call(lambda *refs: front_kernel(sizes, rows, block, *refs), out...  76.9 us
    pallas_call x1, Pallas kernels, middle_part(): pl.pallas_call(lambda *refs: middle_kernel(own, tensor_total, *refs), out...  16.8 us
    unnamed x5, local copies, waits for them, and re-layouts  8.6 us

profile of v1, /device:TPU:0, one launch (start us, length us, event | category | flops | bytes accessed | tf_op | source)
XLA Modules:
  0.0 187.0 jit_solution(11221751991099007809)
XLA Ops:
  0.6 76.9 %front.1 = (bf16[2,2,4,2,64,1024]{5,4,3,2,1,0:T(8,128)(2,1)}, bf16[2,4,2,64,256]{4,3,2,1,0:T(8,128)(2,1)}, bf16[3,4,2,64,256]{4,3,2,1,0:T(8,128)(2,1)}, f32[4,2,...) custom-call(s32[2]{0:T(128)} %refs_0_.5, ...), custom_call_target="tpu_custom_call" | custom-call | tf_op jit(solution)/shard_map/front/pallas_call | solution.py:380
  77.6 16.8 %middle.1 = (f32[2048,128]{1,0:T(8,128)}, f32[512,512]{1,0:T(8,128)}, bf16[2,2,256,256]{3,2,1,0:T(8,128)(2,1)}, bf16[4,512,1024]{2,1,0:T(8,128)(2,1)}, bf16[2,512,256]{2,1,0:T(8,128)(2,1)}, /*index=5*/f32[24,512]{1,0:T(8,128)}) custom-call(s32[2]{0:T(128)} %refs_0_.5, f32[8,8,128]{2,1,0:T(8,128)} %bitcast.56, f32[2048,128]{1,0:T(8,128)} %bitcast.44, ...), custom_call_target="tpu_custom_call" | custom-call | tf_op jit(solution)/shard_map/middle/pallas_call | solution.py:521
  94.4 77.5 %back.1 = (f32[2048,128]{1,0:T(8,128)}, f32[64,512]{1,0:T(8,128)}, f32[64,512]{1,0:T(8,128)}, f32[64,128]{1,0:T(8,128)}, f32[3,64,128]{2,1,0:T(8,128)}, /*index=5*/f32[40,512]{1,0:T(8,128)}) custom-call(s32[2]{0:T(128)} %refs_0_.5, bf16[2,2,256,256]{3,2,1,0:T(8,128)(2,1)} %get-tuple-element.38.refs_1_, bf16[1024,256]{1,0:T(8,128)(2,1)} %get-tuple-element.39.refs_2_, ...), custom_call_target="tpu_custom_call" | custom-call | tf_op jit(solution)/shard_map/back/pallas_call | solution.py:920
  171.9 1.4 fusion
  173.3 1.3 slice_reduce_fusion.1
  174.6 1.4 slice_reduce_fusion
  177.2 2.6 %copy.34 = f32[256,2,512]{2,1,0:T(2,128)} copy(f32[256,2,512]{2,1,0:T(2,128)} %bitcast.48) | data formatting | bytes 2097152
  179.8 1.5 copy.35
  181.3 1.4 copy.36
  182.7 1.6 copy.37
  184.3 1.6 copy.38

commit v2 on v1

v2 whole, which is shorter than its diff:
```python
import math

import jax
import jax.numpy as jnp
import numpy as np
from jax import lax
from jax.experimental import pallas as pl
from jax.experimental.pallas import tpu as pltpu
from jax.sharding import PartitionSpec as P

HD = 64
F32 = jnp.float32
BF16 = jnp.bfloat16
MESH = pl.DeviceIdType.MESH
VMEM_LIMIT = 60 * 1024 * 1024

NN = (((1,), (0,)), ((), ()))
NT = (((1,), (1,)), ((), ()))


def dot(a, b, dims=NN):
    return lax.dot_general(a, b, dims, preferred_element_type=F32)


class Place:
    def __init__(self, sizes):
        dp, tensor = lax.axis_index("dp"), lax.axis_index("tensor")
        self.sizes = sizes
        self.at = {"z": dp // sizes["y"], "y": dp % sizes["y"], "x": tensor // 2, "c": tensor % 2}

    def moved(self, axis, delta):
        size = self.sizes[axis]
        if size == 2:
            return 1 - self.at[axis]
        return lax.rem(self.at[axis] + (delta % size), size)

    def device(self, **moves):
        at = dict(self.at)
        for axis, delta in moves.items():
            at[axis] = self.moved(axis, delta)
        return (at["z"] * self.sizes["y"] + at["y"], at["x"] * 2 + at["c"])

    def peers(self):
        out = [self.device(x=1), self.device(c=1), self.device(x=1, c=1), self.device(y=1)]
        out += [self.device(z=delta) for delta in range(1, self.sizes["z"])]
        return out

    def meet(self):
        barrier = pltpu.get_barrier_semaphore()
        peers = self.peers()
        for peer in peers:
            pl.semaphore_signal(barrier, inc=1, device_id=peer, device_id_type=MESH)
        return lambda: pl.semaphore_wait(barrier, len(peers))


def remote(src, dst, send, recv, device):
    return pltpu.make_async_remote_copy(
        src_ref=src, dst_ref=dst, send_sem=send, recv_sem=recv, device_id=device, device_id_type=MESH
    )


def steps_of(sizes, order):
    out = []
    for axis in order:
        out += ["z1", "z2"] if axis == "z" and sizes["z"] == 4 else [axis]
    return out


def slots_of(sizes, order):
    return sum(2 if step in ("z1", "z2") else sizes[step] - 1 for step in steps_of(sizes, order))


class Gather:
    def __init__(self, place, view, order, rows, send, recv, base):
        self.place, self.view, self.order = place, view, order
        self.send, self.recv, self.base = send, recv, base
        self.low, self.high = pl.ds(0, rows // 2), pl.ds(rows // 2, rows // 2)
        self.steps = steps_of(place.sizes, order)

    def part(self, step, **changed):
        where = dict(self.place.at)
        where["r"] = slice(None)
        for axis in self.order[: self.order.index(self.steps[step][0])]:
            where[axis] = slice(None)
        where.update(changed)
        return self.view(where)

    def copies(self, step):
        name, moved = self.steps[step], self.place.moved
        if name == "z1":
            return [(self.part(step), self.part(step, z=moved("z", -d)), {"z": d}) for d in (1, -1)]
        if name == "z2":
            out = []
            for d, rows in ((1, self.low), (-1, self.high)):
                far = self.part(step, z=moved("z", 2), r=rows)
                out.append((self.part(step, z=moved("z", -d), r=rows), far, {"z": d}))
            return out
        size = self.place.sizes[name]
        return [
            (self.part(step), self.part(step, **{name: moved(name, -d)}), {name: d}) for d in range(1, size)
        ]

    def made(self, step, came):
        slot = self.base
        for index in range(step):
            slot += len(self.copies(index))
        for source, landed, moves in self.copies(step):
            ref = landed if came else source
            yield remote(ref, ref, self.send.at[slot], self.recv.at[slot], self.place.device(**moves))
            slot += 1

    def start(self, step):
        for copy in self.made(step, False):
            copy.start()

    def arrive(self, step):
        for copy in self.made(step, True):
            copy.wait_recv()

    def next(self, step):
        if 0 < step <= len(self.steps):
            self.arrive(step - 1)
        if step < len(self.steps):
            self.start(step)

    def finish(self):
        for step in range(len(self.steps)):
            for copy in self.made(step, False):
                copy.wait_send()


def lanes(shape, limit):
    return lax.broadcasted_iota(jnp.int32, shape, 1) < limit


def token_rows(ref, seq, rows):
    return [ref[pl.ds(2 * j + seq, rows, stride=8), :] for j in range(4)]


def row_mean(parts):
    total = parts[0]
    for part in parts[1:]:
        total = total + part
    return jnp.sum(total, -1, keepdims=True) * (1.0 / (128 * len(parts)))


def normalize(parts):
    mean = row_mean(parts)
    center = [part - mean for part in parts]
    spread = row_mean([part * part for part in center])
    scale = lax.rsqrt(spread + 1e-05)
    return center, scale


def rope(value, cos, sin_a, sin_b):
    return value * cos + pltpu.roll(value, 96, 1) * sin_a + pltpu.roll(value, 32, 1) * sin_b


def rope_back(grad, cos, sin_a, sin_b):
    return grad * cos - pltpu.roll(grad, 96, 1) * sin_a - pltpu.roll(grad, 32, 1) * sin_b


def rope_tables(rows):
    half = HD // 2
    rates = np.exp(np.arange(half, dtype=np.float32) * np.float32(-2.0 * math.log(10000.0) / HD))
    angles = np.arange(rows, dtype=np.float32)[:, None] * rates.astype(np.float32)[None, :]
    cos, sin, zero = np.cos(angles), np.sin(angles), np.zeros_like(angles)
    tables = [[cos] * 4, [-sin, zero] * 2, [zero, sin] * 2]
    return jnp.asarray(np.stack([np.concatenate(table, -1) for table in tables]).astype(np.float32))


FRONT = (("q", "xzy"), ("k", "zyx"), ("v", "yxz"), ("n", "zy"), ("out", "xyzc"), ("u0", "xyzc"), ("u1", "xyzc"), ("d0", "xyzc"), ("d1", "zxyc"))


def x_lane(index):
    return index if isinstance(index, slice) else pl.ds(pl.multiple_of(index * 128, 128), 128)


def front_kernel(
    sizes,
    rows,
    block,
    lengths,
    x_ref,
    qkv_shard,
    out_shard,
    up_shard,
    down_shard,
    gain,
    shift,
    tables,
    ff_all,
    out_all,
    qkv_all,
    counts,
    normed_all,
    q_all,
    k_all,
    v_all,
    lse,
    attended,
    own_normed,
    own_attended,
    local_sem,
    send,
    recv,
    send_n,
    recv_n,
    send_a,
    recv_a,
):
    place = Place(sizes)
    at = place.at
    x, c, z, y = at["x"], at["c"], at["z"], at["y"]
    t = x * 2 + c
    own = rows // 4
    shard = qkv_shard.shape[1]
    met = place.meet()

    def local(index, src, dst):
        copy = pltpu.make_async_copy(src, dst, local_sem.at[index])
        copy.start()
        return copy

    def row_block(index):
        return pl.ds(pl.multiple_of(index * own, own), own)

    def qkv_view(i):
        return lambda w: qkv_all.at[i, w["z"], w["y"], w["r"], x_lane(w["x"])]

    def ff_view(start):
        return lambda w: ff_all.at[w["x"], w["c"], w["z"], w["y"], w["r"], pl.ds(start, 256)]

    views = {
        "q": qkv_view(0),
        "k": qkv_view(1),
        "v": qkv_view(2),
        "n": lambda w: counts.at[w["z"], w["y"], w["r"]],
        "out": lambda w: out_all.at[w["c"], w["z"], w["y"], w["r"], x_lane(w["x"])],
        "u0": ff_view(0),
        "u1": ff_view(256),
        "d0": ff_view(512),
        "d1": ff_view(768),
    }
    plans = {}
    base = 0
    for name, order in FRONT:
        plans[name] = Gather(place, views[name], order, 16 if name == "n" else shard, send, recv, base)
        base += slots_of(sizes, order)

    def go(names, step):
        for name in names:
            plans[name].next(step)

    copies = [
        local(0, qkv_shard, qkv_all.at[:, z, y, :, x_lane(x)]),
        local(1, out_shard, out_all.at[c, z, y, :, x_lane(x)]),
        local(2, up_shard, ff_all.at[x, c, z, y, :, pl.ds(0, 512)]),
        local(3, down_shard, ff_all.at[x, c, z, y, :, pl.ds(512, 512)]),
    ]
    total = lengths[0] + lengths[1]
    counts[z, y] = jnp.full((16, 128), total.astype(F32))
    copies[0].wait()
    met()
    heads, ff = ("q", "k", "v"), ("u0", "d0", "out", "u1", "d1")
    go(heads, 0)
    go("n", 0)
    for s in range(2):
        center, scale = normalize(token_rows(x_ref, s, own))
        for j in range(4):
            lane = pl.ds(128 * j, 128)
            value = center[j] * scale * gain[:, lane] + shift[:, lane]
            own_normed[s, :, lane] = value.astype(BF16)
    mine = row_block(t)

    def tokens(index, ref, moves):
        return remote(ref, ref, send_n.at[index], recv_n.at[index], place.device(**moves))

    sent = [
        remote(own_normed.at[1 - x], normed_all.at[mine], send_n.at[0], recv_n.at[0], place.device(x=1)),
        remote(own_normed.at[x], normed_all.at[mine], send_n.at[1], recv_n.at[1], place.device(c=1)),
    ]
    for copy in sent:
        copy.start()
    keep = local(0, own_normed.at[x], normed_all.at[mine])
    for copy in copies[1:]:
        copy.wait()
    go(heads, 1)
    go("n", 1)
    go(ff, 0)
    go(heads, 2)
    go(ff[:2], 1)
    far = normed_all.at[row_block((1 - x) * 2 + c)]
    tokens(0, far, {"x": 1}).wait_recv()
    sent.append(tokens(2, far, {"c": 1}))
    sent[-1].start()
    go(heads, 3)
    go("n", 2)
    go(ff[2:], 1)
    keep.wait()
    tokens(1, normed_all.at[row_block(x * 2 + 1 - c)], {"c": 1}).wait_recv()
    go(heads, 4)
    tokens(2, normed_all.at[row_block((1 - x) * 2 + 1 - c)], {"c": 1}).wait_recv()
    go(ff, 2)

    w_qkv = [qkv_all[i].reshape(-1, 256) for i in range(3)]

    def project(index, carry):
        here = pl.ds(pl.multiple_of(index * block, block), block)
        normed = normed_all[here, :]
        cos, sin_a, sin_b = (tables[i, here, :] for i in range(3))
        for i, ref in ((0, q_all), (1, k_all), (2, v_all)):
            value = dot(normed, w_qkv[i])
            for pair in range(2):
                lane = pl.ds(128 * pair, 128)
                part = value[:, 128 * pair : 128 * pair + 128]
                if i < 2:
                    part = rope(part, cos, sin_a, sin_b)
                if i == 0:
                    part = part.astype(BF16) * jnp.asarray(HD**-0.5, BF16)
                ref[here, lane] = part.astype(BF16)
        return carry

    lax.fori_loop(0, rows // block, project, 0)
    go("n", 3)
    go(ff[:2], 3)

    length = lengths[x]
    half = lanes((block, 128), HD)
    zero = jnp.zeros((block, 128), BF16)
    blocks = rows // block

    def hand(qb, act):
        to = {"x": qb // 2, "c": qb % 2}
        source, target = own_attended.at[pl.ds(qb * block, block)], attended.at[c, x]
        device = (lax.axis_index("dp"), jnp.asarray(qb, jnp.int32))

        @pl.when(t != qb)
        def _():
            copy = remote(source, target, send_a.at[qb], recv_a.at[t], device)
            if act == "start":
                copy.start()
            else:
                copy.wait_send()

        if act == "start":

            @pl.when(t == qb)
            def _():
                pltpu.make_async_copy(source, target, recv_a.at[t]).start()

    for qb in range(blocks):
        here = pl.ds(qb * block, block)
        keys = (qb + 1) * block
        key_pos = lax.broadcasted_iota(jnp.int32, (block, keys), 1)
        query_pos = lax.broadcasted_iota(jnp.int32, (block, keys), 0) + qb * block
        allowed = key_pos <= query_pos
        if keys > rows // 2:
            allowed = allowed & (key_pos < length)

        def attend(pair, carry, here=here, keys=keys, allowed=allowed):
            lane = pl.ds(pl.multiple_of(pair * 128, 128), 128)
            queries = q_all[here, lane]
            k_part = k_all[pl.ds(0, keys), lane]
            v_part = v_all[pl.ds(0, keys), lane]
            mixed = []
            for head in range(2):
                masked = jnp.where(half, queries, zero) if head == 0 else jnp.where(half, zero, queries)
                scores = jnp.where(allowed, dot(masked, k_part, NT), -1e30)
                highest = jnp.max(scores, -1, keepdims=True)
                expd = jnp.exp(scores - highest)
                denom = jnp.sum(expd, -1, keepdims=True)
                probs = (expd * (1.0 / denom)).astype(BF16)
                mixed.append(dot(probs, v_part))
                wide = jnp.broadcast_to(highest + jnp.log(denom), (block, 128))
                lse[pair * 2 + head, :, here] = jnp.transpose(wide)[:8]
            own_attended[here, lane] = jnp.where(half, mixed[0], mixed[1]).astype(BF16)
            return carry

        lax.fori_loop(0, 2, attend, 0)
        hand(qb, "start")
        if qb == 1:
            go(ff[2:], 3)
        if qb == 2:
            go(ff[:2], 4)
    go(ff[2:], 4)
    for k in range(2):
        for s in range(2):
            came = attended.at[k, s]
            index = s * 2 + k
            remote(came, came, send_a.at[0], recv_a.at[index], place.device(x=1)).wait_recv()
    go(ff, 5)
    for plan in plans.values():
        plan.finish()
    for copy in sent:
        copy.wait_send()
    for qb in range(blocks):
        hand(qb, "finish")


def front(sizes, rows, lengths, x, qkv, out, up, down, gain, shift, tables):
    zs, ys = sizes["z"], sizes["y"]
    shard = qkv.shape[1]
    own = rows // 4
    slots = sum(slots_of(sizes, order) for _, order in FRONT)
    any_spec = pl.BlockSpec(memory_space=pl.ANY)
    vmem = pl.BlockSpec(memory_space=pltpu.VMEM)
    shapes = [
        ((2, 2, zs, ys, shard, 1024), BF16),
        ((2, zs, ys, shard, 256), BF16),
        ((3, zs, ys, shard, 256), BF16),
        ((zs, ys, 16, 128), F32),
        ((rows, 512), BF16),
        ((rows, 256), BF16),
        ((rows, 256), BF16),
        ((rows, 256), BF16),
        ((4, 8, rows), F32),
        ((2, 2, own, 256), BF16),
    ]
    return pl.pallas_call(
        lambda *refs: front_kernel(sizes, rows, own, *refs),
        out_shape=[jax.ShapeDtypeStruct(*shape) for shape in shapes],
        in_specs=[pl.BlockSpec(memory_space=pltpu.SMEM), vmem] + [any_spec] * 4 + [vmem] * 3,
        out_specs=[vmem] * len(shapes),
        scratch_shapes=[
            pltpu.VMEM((2, own, 512), BF16),
            pltpu.VMEM((rows, 256), BF16),
            pltpu.SemaphoreType.DMA((4,)),
            pltpu.SemaphoreType.DMA((slots,)),
            pltpu.SemaphoreType.DMA((slots,)),
            pltpu.SemaphoreType.DMA((3,)),
            pltpu.SemaphoreType.DMA((3,)),
            pltpu.SemaphoreType.DMA((4,)),
            pltpu.SemaphoreType.DMA((4,)),
        ],
        name="front",
        compiler_params=pltpu.CompilerParams(
            collective_id=0, has_side_effects=True, vmem_limit_bytes=VMEM_LIMIT
        ),
    )(lengths, x, qkv, out, up, down, gain, shift, tables)


def gelu_parts(value):
    cdf = 0.5 + 0.5 * lax.erf(value * (2.0**-0.5))
    density = jnp.exp(-0.5 * value * value) * ((2.0 * math.pi) ** -0.5)
    return value * cdf, cdf + value * density


def middle_kernel(
    own,
    tensor_total,
    lengths,
    counts,
    x_ref,
    teacher,
    cotangent,
    attended,
    ff_all,
    out_all,
    gain,
    shift,
    output,
    grad_middle,
    grad_attended,
    grad_ff,
    grad_out,
    stats,
    middle,
    seed,
    slope,
    hidden,
    total_sum,
):
    tokens = 2 * own
    tensor = lax.axis_index("tensor")
    count = jnp.sum(counts[...], axis=0)[0:1]
    factor = tensor_total / count
    valid = []
    for s in range(2):
        rows = pl.ds(s * own, own)
        attn = dot(attended[0, s], out_all[0], NT) + dot(attended[1, s], out_all[1], NT)
        parts = token_rows(x_ref, s, own)
        for j in range(4):
            middle[rows, pl.ds(128 * j, 128)] = parts[j] + attn[:, 128 * j : 128 * j + 128]
        position = tensor * own + lax.broadcasted_iota(jnp.int32, (own, 128), 0)
        valid.append((position < lengths[s]).astype(F32))
    value = middle[...]
    mean = jnp.mean(value, -1, keepdims=True)
    center = value - mean
    scale = lax.rsqrt(jnp.mean(center * center, -1, keepdims=True) + 1e-05)
    normed = (center * scale * gain[...] + shift[...]).astype(BF16)
    normed_t = jnp.transpose(normed)

    total_sum[...] = jnp.zeros_like(total_sum)

    def up(t, carry):
        before = dot(normed, ff_all[t, :, pl.ds(0, 512)])
        act, slope_t = gelu_parts(before)
        act = act.astype(BF16)
        slope[t] = slope_t
        hidden[t] = act
        total_sum[...] += dot(act, ff_all[t, :, pl.ds(512, 512)], NT)
        return carry

    lax.fori_loop(0, 4, up, 0)

    square = jnp.zeros((own, 128), F32)
    for s in range(2):
        rows = pl.ds(s * own, own)
        want = token_rows(teacher, s, own)
        weight = token_rows(cotangent, s, own)
        for j in range(4):
            lane = pl.ds(128 * j, 128)
            out = middle[rows, lane] + total_sum[rows, lane]
            output[pl.ds(2 * j + s, own, stride=8), :] = out
            differ = out - want[j]
            square = square + valid[s] * differ * differ
            seed[rows, lane] = factor * valid[s] * (weight[j] + differ)
    grad_f = seed[...].astype(BF16)
    grad_f_t = jnp.transpose(grad_f)
    total_sum[...] = jnp.zeros_like(total_sum)

    def down(t, carry):
        grad_hidden = dot(grad_f, ff_all[t, :, pl.ds(512, 512)])
        grad_before = (slope[t] * grad_hidden).astype(BF16)
        grad_ff[t, :, pl.ds(0, 512)] = dot(normed_t, grad_before).astype(BF16)
        grad_ff[t, :, pl.ds(512, 512)] = dot(grad_f_t, hidden[t]).astype(BF16)
        total_sum[...] += dot(grad_before, ff_all[t, :, pl.ds(0, 512)], NT)
        return carry

    lax.fori_loop(0, 4, down, 0)

    grad_normed = total_sum[...]
    unit = (middle[...] - mean) * scale
    stats[...] = jnp.zeros_like(stats)
    stats[0:1, 0:128] = jnp.sum(square, 0, keepdims=True)
    stats[8:9] = jnp.sum(grad_normed * unit, 0, keepdims=True)
    stats[16:17] = jnp.sum(grad_normed, 0, keepdims=True)
    scaled = grad_normed * gain[...]
    inner = jnp.mean(scaled * unit, -1, keepdims=True)
    grad = seed[...] + scale * (scaled - jnp.mean(scaled, -1, keepdims=True) - unit * inner)
    grad_middle[...] = grad
    branch = grad.astype(BF16)
    branch_t = jnp.transpose(branch)
    for k in range(2):
        grad_out[k] = (dot(branch_t[:, :own], attended[k, 0]) + dot(branch_t[:, own:], attended[k, 1])).astype(BF16)
        back = dot(branch, out_all[k]).astype(BF16)
        for s in range(2):
            grad_attended[k, s] = back[s * own : s * own + own]


def middle_part(own, tensor_total, lengths, counts, x, teacher, cotangent, attended, ff_all, out_all, gain, shift):
    tokens = 2 * own
    vmem = pl.BlockSpec(memory_space=pltpu.VMEM)
    shapes = [
        (x.shape, F32),
        ((tokens, 512), F32),
        ((2, 2, own, 256), BF16),
        ((4, 512, 1024), BF16),
        ((2, 512, 256), BF16),
        ((24, 512), F32),
    ]
    return pl.pallas_call(
        lambda *refs: middle_kernel(own, tensor_total, *refs),
        out_shape=[jax.ShapeDtypeStruct(*shape) for shape in shapes],
        in_specs=[pl.BlockSpec(memory_space=pltpu.SMEM)] + [vmem] * 9,
        out_specs=[vmem] * len(shapes),
        scratch_shapes=[
            pltpu.VMEM((tokens, 512), F32),
            pltpu.VMEM((tokens, 512), F32),
            pltpu.VMEM((4, tokens, 512), F32),
            pltpu.VMEM((4, tokens, 512), BF16),
            pltpu.VMEM((tokens, 512), F32),
        ],
        name="middle",
        compiler_params=pltpu.CompilerParams(vmem_limit_bytes=VMEM_LIMIT),
    )(lengths, counts, x, teacher, cotangent, attended, ff_all, out_all, gain, shift)


class Scatter:
    def __init__(self, place, view, work, order, dims, rows, lead, landing, final, send, recv, base):
        self.place, self.view, self.work, self.order, self.dims = place, view, work, order, dims
        self.lead, self.landing, self.final = lead, landing, final
        self.send, self.recv, self.base = send, recv, base
        self.low, self.high = pl.ds(0, rows // 2), pl.ds(rows // 2, rows // 2)
        self.steps = steps_of(place.sizes, order)

    def done(self, step):
        return self.order[: self.order.index(self.steps[step][0])]

    def part(self, step, kept=False, **changed):
        where = dict(self.place.at)
        where["r"] = slice(None)
        for axis in self.order:
            if axis not in self.done(step):
                where[axis] = slice(None)
        where.update(changed)
        return (self.work if kept or step > 0 else self.view)(where)

    def sends(self, step):
        name, moved = self.steps[step], self.place.moved
        if name == "z1":
            return [({"z": moved("z", 2), "r": rows}, {"z": d}) for d, rows in ((1, self.low), (-1, self.high))]
        if name == "z2":
            return [({"z": moved("z", d)}, {"z": d}) for d in (1, -1)]
        return [({name: moved(name, d)}, {name: d}) for d in range(1, self.place.sizes[name])]

    def sums(self, step):
        name, moved = self.steps[step], self.place.moved
        if name == "z1":
            return [({"z": moved("z", 1), "r": self.low}, [0]), ({"z": moved("z", -1), "r": self.high}, [1])]
        return [({name[0]: self.place.at[name[0]]}, list(range(len(self.sends(step)))))]

    def made(self, step):
        slot = self.base
        for index in range(step):
            slot += len(self.sends(index))
        for index, (where, moves) in enumerate(self.sends(step)):
            yield remote(
                self.part(step, **where),
                self.landing[step].at[index],
                self.send.at[slot + index],
                self.recv.at[slot + index],
                self.place.device(**moves),
            )

    def start(self, step):
        for copy in self.made(step):
            copy.start()

    def arrive(self, step):
        for copy in self.made(step):
            copy.wait_recv()
        axis = self.steps[step][0]
        rest = [a for a in self.dims if a in self.order and a not in self.done(step) and a != axis]
        sizes = [self.place.sizes[a] for a in rest]
        landing = self.landing[step]
        last = step == len(self.steps) - 1
        for where, pieces in self.sums(step):

            def add(index, carry, where=where, pieces=pieces):
                chosen = {}
                for a, size in zip(reversed(rest), reversed(sizes)):
                    chosen[a] = lax.rem(index, size)
                    index = index // size
                total = self.part(step, **chosen, **where)[...].astype(F32)
                for piece in pieces:
                    place = (piece,) + (slice(None),) * self.lead + tuple(chosen[a] for a in rest)
                    total = total + landing[place].astype(F32)
                if last:
                    self.final[...] = total
                else:
                    self.part(step, kept=True, **chosen, **where)[...] = total.astype(BF16)
                return carry

            count = math.prod(sizes)
            if count == 1:
                add(0, 0)
            else:
                lax.fori_loop(0, count, add, 0)

    def next(self, step):
        if 0 < step <= len(self.steps):
            self.arrive(step - 1)
        if step < len(self.steps):
            self.start(step)

    def finish(self):
        for step in range(len(self.steps)):
            for copy in self.made(step):
                copy.wait_send()


def landing_shapes(sizes, order, dims, rows, width, lead=(), lane_x=False):
    left = list(order)
    shapes = []
    for step in steps_of(sizes, order):
        axis = step[0]
        if step != "z2" and axis in left:
            left.remove(axis)
        count = 2 if step in ("z1", "z2") else sizes[axis] - 1
        high = rows // 2 if step == "z1" else rows
        wide = width * 2 if lane_x and "x" in left else width
        shapes.append((count,) + lead + tuple(sizes[a] for a in dims if a in left) + (high, wide))
    return shapes


BACK = (
    ("u0", "czyx", "xczy", 256, False),
    ("u1", "czyx", "xczy", 256, False),
    ("d0", "czyx", "xczy", 256, False),
    ("d1", "cyxz", "xczy", 256, False),
    ("out", "czyx", "czy", 128, True),
    ("q", "yzx", "zy", 128, True),
    ("k", "xyz", "zy", 128, True),
    ("v", "zxy", "zy", 128, True),
)


def back_kernel(
    sizes,
    rows,
    block,
    shard,
    lengths,
    grad_attended,
    q_all,
    k_all,
    v_all,
    lse,
    normed_all,
    qkv_all,
    grad_middle,
    x_ref,
    gain,
    tables,
    grad_ff,
    grad_out,
    stats,
    grad_inputs,
    up_final,
    down_final,
    out_final,
    qkv_final,
    stats_final,
    g_all,
    k_t,
    grad_q,
    grad_k,
    grad_v,
    grad_proj,
    grad_qkv,
    grad_n,
    ff_work,
    out_work,
    from_core,
    to_x,
    from_x,
    stat_send,
    stat_land,
    send,
    recv,
    send_g,
    recv_g,
    send_n,
    recv_n,
    send_s,
    recv_s,
    *landing,
):
    place = Place(sizes)
    at = place.at
    x, c, z, y = at["x"], at["c"], at["z"], at["y"]
    t = x * 2 + c
    own = rows // 4
    blocks = rows // block
    met = place.meet()

    def row_block(index):
        return pl.ds(pl.multiple_of(index * own, own), own)

    def ff_view(start):
        return lambda w: grad_ff.at[w["x"], w["c"], w["z"], w["y"], w["r"], pl.ds(start, 256)]

    def ff_kept(start):
        return lambda w: ff_work.at[w["x"], w["z"], w["y"], w["r"], pl.ds(start, 256)]

    def qkv_view(i):
        return lambda w: grad_qkv.at[i, w["z"], w["y"], w["r"], x_lane(w["x"])]

    views = {
        "u0": (ff_view(0), ff_kept(0), up_final.at[:, pl.ds(0, 256)]),
        "u1": (ff_view(256), ff_kept(256), up_final.at[:, pl.ds(256, 256)]),
        "d0": (ff_view(512), ff_kept(512), down_final.at[:, pl.ds(0, 256)]),
        "d1": (ff_view(768), ff_kept(768), down_final.at[:, pl.ds(256, 256)]),
        "out": (
            lambda w: grad_out.at[w["c"], w["z"], w["y"], w["r"], x_lane(w["x"])],
            lambda w: out_work.at[w["z"], w["y"], w["r"], x_lane(w["x"])],
            out_final,
        ),
    }
    for i, name in enumerate("qkv"):
        views[name] = (qkv_view(i), qkv_view(i), qkv_final.at[i])
    plans = {}
    base = 0
    used = 0
    for name, order, dims, width, lane_x in BACK:
        view, kept, final = views[name]
        count = len(steps_of(sizes, order))
        plans[name] = Scatter(
            place, view, kept, order, dims, shard, 0, landing[used : used + count], final, send, recv, base
        )
        used += count
        base += slots_of(sizes, order)

    def go(names, step):
        for name in names:
            plans[name].next(step)

    met()
    moved = []
    for moves in ({"x": 1}, {"x": 1, "c": 1}, {"c": 1}):
        to = dict(at)
        for axis in moves:
            to[axis] = 1 - at[axis]
        copy = remote(
            grad_attended.at[to["c"], to["x"]],
            g_all.at[row_block(t)],
            send_g.at[len(moved)],
            recv_g.at[t],
            place.device(**moves),
        )
        copy.start()
        moved.append(copy)
    pltpu.make_async_copy(grad_attended.at[c, x], g_all.at[row_block(t)], recv_g.at[t]).start()
    ff = ("u0", "d0", "u1", "d1", "out")
    go(ff, 0)
    for pair in range(2):
        k_t[pair] = jnp.transpose(k_all[:, pl.ds(128 * pair, 128)])
    normed_t = jnp.transpose(normed_all[...])
    go(ff[:2], 1)

    length = lengths[x]
    half = lanes((block, 128), HD)
    zero = jnp.zeros((block, 128), BF16)
    upper = lax.broadcasted_iota(jnp.int32, (128, block), 0) < HD

    def to_core(qb, act):
        @pl.when(c != qb % 2)
        def _():
            copy = remote(
                grad_n.at[pl.ds(qb * block, block)],
                from_core.at[qb // 2],
                send_n.at[qb // 2],
                recv_n.at[qb // 2],
                place.device(c=1),
            )
            copy.start() if act == "start" else copy.wait_send()

    def arrived(index):
        slot = from_core.at[index]
        remote(slot, slot, send_n.at[index], recv_n.at[index], place.device(c=1)).wait_recv()

    def cross():
        return remote(to_x, from_x, send_n.at[2], recv_n.at[2], place.device(x=1))

    def to_chip(qb):
        @pl.when((c == qb % 2) & (x != qb // 2))
        def _():
            arrived(qb // 2)
            to_x[...] = (grad_n[pl.ds(qb * block, block), :] + from_core[qb // 2]).astype(BF16)
            cross().start()

    for qb in range(blocks - 1, -1, -1):
        here = pl.ds(qb * block, block)
        keys = (qb + 1) * block
        seen = pl.ds(0, keys)
        key_pos = lax.broadcasted_iota(jnp.int32, (keys, block), 0)
        query_pos = lax.broadcasted_iota(jnp.int32, (keys, block), 1) + qb * block
        allowed = key_pos <= query_pos
        if keys > rows // 2:
            allowed = allowed & (key_pos < length)
        came = g_all.at[here]
        remote(came, came, send_g.at[0], recv_g.at[qb], place.device(x=1)).wait_recv()

        def attend(pair, carry, qb=qb, here=here, seen=seen, keys=keys, allowed=allowed):
            lane = pl.ds(pl.multiple_of(pair * 128, 128), 128)
            queries = q_all[here, lane]
            grads = g_all[here, lane]
            k_part = k_all[seen, lane]
            v_part = v_all[seen, lane]
            dq = []
            for head in range(2):
                if head == 0:
                    q_m, g_m = jnp.where(half, queries, zero), jnp.where(half, grads, zero)
                else:
                    q_m, g_m = jnp.where(half, zero, queries), jnp.where(half, zero, grads)
                scores = dot(k_part, q_m, NT)
                probs = jnp.where(allowed, jnp.exp(scores - lse[pair * 2 + head, 0:1, here]), 0.0)
                grad_probs = dot(v_part, g_m, NT)
                inner = jnp.sum(probs * grad_probs, 0, keepdims=True)
                grad_raw = (probs * (grad_probs - inner)).astype(BF16)
                add_k = dot(grad_raw, q_m)
                add_v = dot(probs.astype(BF16), g_m)
                if qb == blocks - 1 and head == 0:
                    grad_k[seen, lane] = add_k
                    grad_v[seen, lane] = add_v
                else:
                    grad_k[seen, lane] += add_k
                    grad_v[seen, lane] += add_v
                dq.append(dot(k_t[pair, :, seen], grad_raw))
            grad_q[here, lane] = jnp.transpose(jnp.where(upper, dq[0], dq[1])) * HD**-0.5
            return carry

        lax.fori_loop(0, 2, attend, 0)

        cos, sin_a, sin_b = (tables[i, here, :] for i in range(3))
        total = jnp.zeros((block, 512), F32)
        for i, ref in ((0, grad_q), (1, grad_k), (2, grad_v)):
            for pair in range(2):
                lane = pl.ds(128 * pair, 128)
                part = ref[here, lane]
                if i < 2:
                    part = rope_back(part, cos, sin_a, sin_b)
                grad_proj[i, here, lane] = part.astype(BF16)
            total = total + dot(grad_proj[i, here, :], qkv_all[i], NT)
        grad_n[here, :] = total
        to_core(qb, "start")
        if qb < blocks - 1:
            to_chip(qb + 1)
        if qb == blocks - 1:
            go(ff[2:], 1)
            go(ff[:2], 2)
        if qb == blocks - 2:
            go(ff[2:], 2)
            go(ff[:2], 3)
        if qb == blocks - 3:
            go(ff[2:], 3)
            go(ff[:2], 4)
    deep = sizes["z"] * sizes["y"]
    for i, name in enumerate("qkv"):
        value = dot(normed_t, grad_proj[i]).astype(BF16)
        grad_qkv[i] = value.reshape(sizes["z"], sizes["y"], shard, 256)
        go(name, 0)
        if i == 0:
            to_chip(0)
    go(ff[2:], 4)
    go(ff[:2], 5)
    stat_send[0] = jnp.zeros_like(stat_send[0])
    stat_send[0, 0:24] = stats[...]
    arrived_own = x
    slot = from_core.at[arrived_own]
    remote(slot, slot, send_n.at[0], recv_n.at[arrived_own], place.device(c=1)).wait_recv()
    cross().wait_recv()
    go("qkv", 1)
    grad_gain = [jnp.zeros((1, 128), F32)] * 4
    grad_shift = [jnp.zeros((1, 128), F32)] * 4
    for s in range(2):
        center, scale = normalize(token_rows(x_ref, s, own))
        near = grad_n[row_block(t), :] + from_core[x]
        chosen = jnp.where(x == s, near, from_x[...].astype(F32))
        grads = [chosen[:, 128 * j : 128 * j + 128] for j in range(4)]
        units = [part * scale for part in center]
        scaled = [grads[j] * gain[:, pl.ds(128 * j, 128)] for j in range(4)]
        mean = row_mean(scaled)
        inner = row_mean([scaled[j] * units[j] for j in range(4)])
        for j in range(4):
            part = grad_middle[pl.ds(s * own, own), pl.ds(128 * j, 128)]
            grad_inputs[pl.ds(2 * j + s, own, stride=8), :] = part + scale * (scaled[j] - mean - units[j] * inner)
            grad_gain[j] = grad_gain[j] + jnp.sum(grads[j] * units[j], 0, keepdims=True)
            grad_shift[j] = grad_shift[j] + jnp.sum(grads[j], 0, keepdims=True)
    for j in range(4):
        stat_send[0, 24:25, 128 * j : 128 * j + 128] = grad_gain[j]
        stat_send[0, 32:33, 128 * j : 128 * j + 128] = grad_shift[j]

    slot = 0
    stat_sent = []
    for phase, axis in enumerate("cxyz"):
        came = []
        for delta in range(1, sizes[axis]):
            copy = remote(
                stat_send.at[phase], stat_land.at[slot], send_s.at[slot], recv_s.at[slot], place.device(**{axis: delta})
            )
            copy.start()
            came.append((copy, slot))
            stat_sent.append(copy)
            slot += 1
        if phase + 2 <= len(plans["q"].steps):
            go("qkv", phase + 2)
        if phase == 1:
            go(ff[2:], 5)
        total = stat_send[phase]
        for copy, index in came:
            copy.wait_recv()
            total = total + stat_land[index]
        if phase < 3:
            stat_send[phase + 1] = total
        else:
            stats_final[...] = total
    for plan in plans.values():
        plan.finish()
    for copy in moved + [cross()] + stat_sent:
        copy.wait_send()
    for qb in range(blocks):
        to_core(qb, "finish")


def back(sizes, rows, lengths, grad_attended, q, k, v, lse, normed, qkv, grad_middle, x, gain, tables, grad_ff, grad_out, stats):
    zs, ys = sizes["z"], sizes["y"]
    shard = 512 // (zs * ys)
    own = rows // 4
    vmem = pl.BlockSpec(memory_space=pltpu.VMEM)
    shapes = [x.shape, (shard, 512), (shard, 512), (shard, 128), (3, shard, 128), (40, 512)]
    lands = []
    for _, order, dims, width, lane_x in BACK:
        lands += landing_shapes(sizes, order, dims, shard, width, lane_x=lane_x)
    slots = sum(slots_of(sizes, item[1]) for item in BACK)
    meets = sum(sizes[axis] - 1 for axis in "cxyz")
    return pl.pallas_call(
        lambda *refs: back_kernel(sizes, rows, own, shard, *refs),
        out_shape=[jax.ShapeDtypeStruct(shape, F32) for shape in shapes],
        in_specs=[pl.BlockSpec(memory_space=pltpu.SMEM)] + [vmem] * 14,
        out_specs=[vmem] * len(shapes),
        scratch_shapes=[
            pltpu.VMEM((rows, 256), BF16),
            pltpu.VMEM((2, 128, rows), BF16),
            pltpu.VMEM((rows, 256), F32),
            pltpu.VMEM((rows, 256), F32),
            pltpu.VMEM((rows, 256), F32),
            pltpu.VMEM((3, rows, 256), BF16),
            pltpu.VMEM((3, zs, ys, shard, 256), BF16),
            pltpu.VMEM((rows, 512), F32),
            pltpu.VMEM((2, zs, ys, shard, 1024), BF16),
            pltpu.VMEM((zs, ys, shard, 256), BF16),
            pltpu.VMEM((2, own, 512), F32),
            pltpu.VMEM((own, 512), BF16),
            pltpu.VMEM((own, 512), BF16),
            pltpu.VMEM((4, 40, 512), F32),
            pltpu.VMEM((meets, 40, 512), F32),
            pltpu.SemaphoreType.DMA((slots,)),
            pltpu.SemaphoreType.DMA((slots,)),
            pltpu.SemaphoreType.DMA((3,)),
            pltpu.SemaphoreType.DMA((4,)),
            pltpu.SemaphoreType.DMA((3,)),
            pltpu.SemaphoreType.DMA((3,)),
            pltpu.SemaphoreType.DMA((meets,)),
            pltpu.SemaphoreType.DMA((meets,)),
        ]
        + [pltpu.VMEM(shape, BF16) for shape in lands],
        name="back",
        compiler_params=pltpu.CompilerParams(
            collective_id=1, has_side_effects=True, vmem_limit_bytes=VMEM_LIMIT
        ),
    )(lengths, grad_attended, q, k, v, lse, normed, qkv, grad_middle, x, gain, tables, grad_ff, grad_out, stats)


def last_kernel(features, counts, grad_inputs, up, down, out, qkv, sums, *outs):
    for source, target in zip((grad_inputs, up, down, out, qkv), outs[:5]):
        target[...] = source[...]
    for target, row in zip(outs[5:9], (24, 32, 8, 16)):
        target[...] = sums[row : row + 1]
    total = jnp.sum(counts[...], axis=0)[0:1, 0:1]
    outs[9][...] = jnp.sum(sums[0:1, 0:128], -1, keepdims=True) / (total * features)


def last(features, counts, grad_inputs, up, down, out, qkv, sums):
    vmem = pl.BlockSpec(memory_space=pltpu.VMEM)
    shapes = [value.shape for value in (grad_inputs, up, down, out, qkv)] + [(1, features)] * 4 + [(1, 1)]
    return pl.pallas_call(
        lambda *refs: last_kernel(features, *refs),
        out_shape=[jax.ShapeDtypeStruct(shape, F32) for shape in shapes],
        in_specs=[vmem] * 7,
        out_specs=[vmem] * len(shapes),
        name="last",
        compiler_params=pltpu.CompilerParams(vmem_limit_bytes=VMEM_LIMIT),
    )(counts, grad_inputs, up, down, out, qkv, sums)


def solution(mesh):
    dp, tensor = mesh.shape["dp"], mesh.shape["tensor"]
    sizes = {"z": dp // 2, "y": 2, "x": tensor // 2, "c": 2}

    def shards(
        inputs, qkv_weight, out_weight, up_weight, down_weight, gain_one, shift_one, gain_two, shift_two, lengths,
        teacher, cotangent,
    ):
        own, sequences, width = inputs.shape
        rows = own * tensor
        shard = width // dp

        def packed(value):
            view = value.reshape(own, sequences, width // 128, 128).transpose(0, 2, 1, 3)
            return view.reshape(own * sequences * (width // 128), 128)

        def unpacked(value):
            view = value.reshape(own, width // 128, sequences, 128).transpose(0, 2, 1, 3)
            return view.reshape(own, sequences, width)

        x = packed(inputs)
        tables = rope_tables(rows)
        ff_all, out_all, qkv_all, counts, normed, q, k, v, lse, attended = front(
            sizes, rows, lengths, x, qkv_weight, out_weight.T, up_weight, down_weight.T, gain_one[None],
            shift_one[None], tables,
        )
        output, grad_middle, grad_attended, grad_ff, grad_out, stats = middle_part(
            own, float(rows * sequences * dp), lengths, counts.reshape(dp, 16, 128), x, packed(teacher),
            packed(cotangent), attended, ff_all.reshape(tensor, width, 1024), out_all.reshape(2, width, 256),
            gain_two[None], shift_two[None],
        )
        grad_inputs, up, down, out, qkv, sums = back(
            sizes, rows, lengths, grad_attended, q, k, v, lse, normed, qkv_all.reshape(3, width, 256), grad_middle, x,
            gain_one[None], tables, grad_ff.reshape(ff_all.shape), grad_out.reshape(out_all.shape), stats,
        )
        grad_inputs, up, down, out, qkv, gain_1, shift_1, gain_2, shift_2, loss = last(
            width, counts.reshape(dp, 16, 128), grad_inputs, up, down, out, qkv, sums
        )
        return (
            unpacked(output), loss.reshape(()), unpacked(grad_inputs), qkv, out.T, up, down.T, gain_1.reshape(width),
            shift_1.reshape(width), gain_2.reshape(width), shift_2.reshape(width),
        )

    tokens, rows_dp, cols_dp = P("tensor", "dp", None), P("dp", "tensor"), P("tensor", "dp")
    heads = P(None, "dp", "tensor")
    return jax.shard_map(
        shards,
        mesh=mesh,
        in_specs=(tokens, heads, cols_dp, rows_dp, cols_dp, P(), P(), P(), P(), P("dp"), tokens, tokens),
        out_specs=(tokens, P(), tokens, heads, cols_dp, rows_dp, cols_dp, P(), P(), P(), P()),
        check_vma=False,
    )
```

time: 188 us -> 156 us (0.83)
  Pallas kernels: 171 us -> 154 us
  local copies, waits for them, and re-layouts: 9.96 us -> 0 us
  other arithmetic: 2.65 us -> 0 us
  between operations: 3.1 us -> 0.83 us
    pallas_call x2 -> x3, Pallas kernels: 154 us -> 138 us  [the longest x1 72.4 us: back(): pl.pallas_call(lambda *refs: back_kernel(sizes, rows, own, shard, *refs),...]
    unnamed x5 -> x0, local copies, waits for them, and re-layouts: 8.6 us -> none
    reduce_sum x2 -> x0, other arithmetic: 2.65 us -> none  [the longest x1 1.37 us: shards(): total = jnp.sum(counts[:, :, 0, 0])]
where the time goes in v2:
time: 156 us; the launch traced here: 155 us
  Pallas kernels  154 us (99%)
    pallas_call x1, Pallas kernels, back(): pl.pallas_call(lambda *refs: back_kernel(sizes, rows, own, shard, *refs),...  72.4 us
    pallas_call x1, Pallas kernels, front(): pl.pallas_call(lambda *refs: front_kernel(sizes, rows, own, *refs), out_s...  62.8 us
    pallas_call x1, Pallas kernels, middle_part(): pl.pallas_call(lambda *refs: middle_kernel(own, tensor_total, *refs), out...  16.8 us

profile of v2, /device:TPU:0, one launch (start us, length us, event | category | flops | bytes accessed | tf_op | source)
XLA Modules:
  0.0 155.3 jit_solution(17141872111303650371)
XLA Ops:
  0.6 62.8 %front.1 = (bf16[2,2,4,2,64,1024]{5,4,3,2,1,0:T(8,128)(2,1)}, bf16[2,4,2,64,256]{4,3,2,1,0:T(8,128)(2,1)}, bf16[3,4,2,64,256]{4,3,2,1,0:T(8,128)(2,1)}, f32[4,2,...) custom-call(s32[2]{0:T(128)} %refs_0_.5, ...), custom_call_target="tpu_custom_call" | custom-call | tf_op jit(solution)/shard_map/front/pallas_call | solution.py:420
  63.5 16.8 %middle.1 = (f32[2048,128]{1,0:T(8,128)}, f32[512,512]{1,0:T(8,128)}, bf16[2,2,256,256]{3,2,1,0:T(8,128)(2,1)}, bf16[4,512,1024]{2,1,0:T(8,128)(2,1)}, bf16[2,512,256]{2,1,0:T(8,128)(2,1)}, /*index=5*/f32[24,512]{1,0:T(8,128)}) custom-call(s32[2]{0:T(128)} %refs_0_.5, f32[8,16,128]{2,1,0:T(8,128)} %bitcast.54, f32[2048,128]{1,0:T(8,128)} %bitcast.45, ...), custom_call_target="tpu_custom_call" | custom-call | tf_op jit(solution)/shard_map/middle/pallas_call | solution.py:563
  80.3 72.4 %back.1 = (f32[2048,128]{1,0:T(8,128)}, f32[64,512]{1,0:T(8,128)}, f32[64,512]{1,0:T(8,128)}, f32[64,128]{1,0:T(8,128)}, f32[3,64,128]{2,1,0:T(8,128)}, /*index=5*/f32[40,512]{1,0:T(8,128)}) custom-call(s32[2]{0:T(128)} %refs_0_.5, bf16[2,2,256,256]{3,2,1,0:T(8,128)(2,1)} %get-tuple-element.48.refs_1_, bf16[1024,256]{1,0:T(8,128)(2,1)} %get-tuple-element.49.refs_2_, ...), custom_call_target="tpu_custom_call" | custom-call | tf_op jit(solution)/shard_map/back/pallas_call | solution.py:999
  152.7 2.5 %last.1 = (f32[2048,128]{1,0:T(8,128)}, f32[64,512]{1,0:T(8,128)}, f32[64,512]{1,0:T(8,128)}, f32[64,128]{1,0:T(8,128)}, f32[3,64,128]{2,1,0:T(8,128)}, /*index=...) custom-call(f32[8,16,128]{2,1,0:T(8,128)} %bitcast.55, ...), custom_call_target="tpu_custom_call" | custom-call | tf_op jit(solution)/shard_map/last/pallas_call | solution.py:1049

commit v3 on v0

v3 whole, which is shorter than its diff:
```python
import math

import jax
import jax.numpy as jnp
import numpy as np
from jax import lax
from jax.experimental import pallas as pl
from jax.experimental.pallas import tpu as pltpu
from jax.sharding import PartitionSpec as P

HD = 64
F32 = jnp.float32
BF16 = jnp.bfloat16
MESH = pl.DeviceIdType.MESH
VMEM_LIMIT = 60 * 1024 * 1024

NN = (((1,), (0,)), ((), ()))
NT = (((1,), (1,)), ((), ()))


def dot(a, b, dims=NN):
    return lax.dot_general(a, b, dims, preferred_element_type=F32)


class Place:
    def __init__(self, sizes):
        dp, tensor = lax.axis_index("dp"), lax.axis_index("tensor")
        self.sizes = sizes
        self.at = {"z": dp // sizes["y"], "y": dp % sizes["y"], "x": tensor // 2, "c": tensor % 2}

    def moved(self, axis, delta):
        size = self.sizes[axis]
        if size == 2:
            return 1 - self.at[axis]
        return lax.rem(self.at[axis] + (delta % size), size)

    def device(self, **moves):
        at = dict(self.at)
        for axis, delta in moves.items():
            at[axis] = self.moved(axis, delta)
        return (at["z"] * self.sizes["y"] + at["y"], at["x"] * 2 + at["c"])

    def peers(self):
        return self.group() + self.across()

    def group(self):
        return [self.device(x=1), self.device(c=1), self.device(x=1, c=1)]

    def across(self):
        out = [self.device(y=1)]
        for delta in range(1, self.sizes["z"]):
            out += [self.device(z=delta), self.device(z=delta, y=1)]
        return out

    def meet(self):
        barrier = pltpu.get_barrier_semaphore()
        peers = self.peers()
        for peer in peers:
            pl.semaphore_signal(barrier, inc=1, device_id=peer, device_id_type=MESH)
        return lambda: pl.semaphore_wait(barrier, len(peers))


def remote(src, dst, send, recv, device):
    return pltpu.make_async_remote_copy(
        src_ref=src, dst_ref=dst, send_sem=send, recv_sem=recv, device_id=device, device_id_type=MESH
    )


def steps_of(sizes, order):
    out = []
    for axis in order:
        out += ["z1", "z2"] if axis == "z" and sizes["z"] == 4 else [axis]
    return out


def slots_of(sizes, order):
    return sum(2 if step in ("z1", "z2") else sizes[step] - 1 for step in steps_of(sizes, order))


class Gather:
    def __init__(self, place, view, order, rows, send, recv, base):
        self.place, self.view, self.order = place, view, order
        self.send, self.recv, self.base = send, recv, base
        self.low, self.high = pl.ds(0, rows // 2), pl.ds(rows // 2, rows // 2)
        self.steps = steps_of(place.sizes, order)

    def part(self, step, **changed):
        where = dict(self.place.at)
        where["r"] = slice(None)
        for axis in self.order[: self.order.index(self.steps[step][0])]:
            where[axis] = slice(None)
        where.update(changed)
        return self.view(where)

    def copies(self, step):
        name, moved = self.steps[step], self.place.moved
        if name == "z1":
            return [(self.part(step), self.part(step, z=moved("z", -d)), {"z": d}) for d in (1, -1)]
        if name == "z2":
            out = []
            for d, rows in ((1, self.low), (-1, self.high)):
                far = self.part(step, z=moved("z", 2), r=rows)
                out.append((self.part(step, z=moved("z", -d), r=rows), far, {"z": d}))
            return out
        size = self.place.sizes[name]
        return [
            (self.part(step), self.part(step, **{name: moved(name, -d)}), {name: d}) for d in range(1, size)
        ]

    def made(self, step, came):
        slot = self.base
        for index in range(step):
            slot += len(self.copies(index))
        for source, landed, moves in self.copies(step):
            ref = landed if came else source
            yield remote(ref, ref, self.send.at[slot], self.recv.at[slot], self.place.device(**moves))
            slot += 1

    def start(self, step):
        for copy in self.made(step, False):
            copy.start()

    def arrive(self, step):
        for copy in self.made(step, True):
            copy.wait_recv()

    def next(self, step):
        if 0 < step <= len(self.steps):
            self.arrive(step - 1)
        if step < len(self.steps):
            self.start(step)

    def finish(self):
        for step in range(len(self.steps)):
            for copy in self.made(step, False):
                copy.wait_send()


def lanes(shape, limit):
    return lax.broadcasted_iota(jnp.int32, shape, 1) < limit


def token_rows(ref, seq, rows):
    return [ref[pl.ds(2 * j + seq, rows, stride=8), :] for j in range(4)]


def row_mean(parts):
    total = parts[0]
    for part in parts[1:]:
        total = total + part
    return jnp.sum(total, -1, keepdims=True) * (1.0 / (128 * len(parts)))


def normalize(parts):
    mean = row_mean(parts)
    center = [part - mean for part in parts]
    spread = row_mean([part * part for part in center])
    scale = lax.rsqrt(spread + 1e-05)
    return center, scale


def rope(value, cos, sin_a, sin_b):
    return value * cos + pltpu.roll(value, 96, 1) * sin_a + pltpu.roll(value, 32, 1) * sin_b


def rope_back(grad, cos, sin_a, sin_b):
    return grad * cos - pltpu.roll(grad, 96, 1) * sin_a - pltpu.roll(grad, 32, 1) * sin_b


def rope_tables(rows):
    half = HD // 2
    rates = np.exp(np.arange(half, dtype=np.float32) * np.float32(-2.0 * math.log(10000.0) / HD))
    angles = np.arange(rows, dtype=np.float32)[:, None] * rates.astype(np.float32)[None, :]
    cos, sin, zero = np.cos(angles), np.sin(angles), np.zeros_like(angles)
    tables = [[cos] * 4, [-sin, zero] * 2, [zero, sin] * 2]
    return jnp.asarray(np.stack([np.concatenate(table, -1) for table in tables]).astype(np.float32))


class Scatter:
    def __init__(self, place, view, work, order, dims, rows, lead, landing, final, send, recv, base):
        self.place, self.view, self.work, self.order, self.dims = place, view, work, order, dims
        self.lead, self.landing, self.final = lead, landing, final
        self.send, self.recv, self.base = send, recv, base
        self.low, self.high = pl.ds(0, rows // 2), pl.ds(rows // 2, rows // 2)
        self.steps = steps_of(place.sizes, order)

    def done(self, step):
        return self.order[: self.order.index(self.steps[step][0])]

    def part(self, step, kept=False, **changed):
        where = dict(self.place.at)
        where["r"] = slice(None)
        for axis in self.order:
            if axis not in self.done(step):
                where[axis] = slice(None)
        where.update(changed)
        return (self.work if kept or step > 0 else self.view)(where)

    def sends(self, step):
        name, moved = self.steps[step], self.place.moved
        if name == "z1":
            return [({"z": moved("z", 2), "r": rows}, {"z": d}) for d, rows in ((1, self.low), (-1, self.high))]
        if name == "z2":
            return [({"z": moved("z", d)}, {"z": d}) for d in (1, -1)]
        return [({name: moved(name, d)}, {name: d}) for d in range(1, self.place.sizes[name])]

    def sums(self, step):
        name, moved = self.steps[step], self.place.moved
        if name == "z1":
            return [({"z": moved("z", 1), "r": self.low}, [0]), ({"z": moved("z", -1), "r": self.high}, [1])]
        return [({name[0]: self.place.at[name[0]]}, list(range(len(self.sends(step)))))]

    def made(self, step):
        slot = self.base
        for index in range(step):
            slot += len(self.sends(index))
        for index, (where, moves) in enumerate(self.sends(step)):
            yield remote(
                self.part(step, **where),
                self.landing[step].at[index],
                self.send.at[slot + index],
                self.recv.at[slot + index],
                self.place.device(**moves),
            )

    def start(self, step):
        for copy in self.made(step):
            copy.start()

    def arrive(self, step):
        for copy in self.made(step):
            copy.wait_recv()
        axis = self.steps[step][0]
        rest = [a for a in self.dims if a in self.order and a not in self.done(step) and a != axis]
        sizes = [self.place.sizes[a] for a in rest]
        landing = self.landing[step]
        last = step == len(self.steps) - 1
        for where, pieces in self.sums(step):

            def add(index, carry, where=where, pieces=pieces):
                chosen = {}
                for a, size in zip(reversed(rest), reversed(sizes)):
                    chosen[a] = lax.rem(index, size)
                    index = index // size
                total = self.part(step, **chosen, **where)[...].astype(F32)
                for piece in pieces:
                    place = (piece,) + (slice(None),) * self.lead + tuple(chosen[a] for a in rest)
                    total = total + landing[place].astype(F32)
                if last:
                    self.final[...] = total
                else:
                    self.part(step, kept=True, **chosen, **where)[...] = total.astype(BF16)
                return carry

            count = math.prod(sizes)
            if count == 1:
                add(0, 0)
            else:
                lax.fori_loop(0, count, add, 0)

    def next(self, step):
        if 0 < step <= len(self.steps):
            self.arrive(step - 1)
        if step < len(self.steps):
            self.start(step)

    def finish(self):
        for step in range(len(self.steps)):
            for copy in self.made(step):
                copy.wait_send()


def landing_shapes(sizes, order, dims, rows, width, lead=(), lane_x=False):
    left = list(order)
    shapes = []
    for step in steps_of(sizes, order):
        axis = step[0]
        if step != "z2" and axis in left:
            left.remove(axis)
        count = 2 if step in ("z1", "z2") else sizes[axis] - 1
        high = rows // 2 if step == "z1" else rows
        wide = width * 2 if lane_x and "x" in left else width
        shapes.append((count,) + lead + tuple(sizes[a] for a in dims if a in left) + (high, wide))
    return shapes


def gelu_parts(value):
    cdf = 0.5 + 0.5 * lax.erf(value * (2.0**-0.5))
    density = jnp.exp(-0.5 * value * value) * ((2.0 * math.pi) ** -0.5)
    return value * cdf, cdf + value * density


GATHERS = (
    ("q", "zyx"),
    ("k", "xzy"),
    ("v", "xyz"),
    ("n", "zy"),
    ("out", "zyxc"),
    ("u0", "xzyc"),
    ("u1", "yzxc"),
    ("d0", "xyzc"),
    ("d1", "xyzc"),
)
SCATTERS = (
    ("d0", "czyx", "xczy", 256, False),
    ("d1", "cxzy", "xczy", 256, False),
    ("u0", "czxy", "xczy", 256, False),
    ("u1", "czyx", "xczy", 256, False),
    ("out", "cyzx", "czy", 128, True),
    ("q", "zyx", "zy", 128, True),
    ("k", "zxy", "zy", 128, True),
    ("v", "yxz", "zy", 128, True),
)
GATHER_AT = dict(
    f0=dict(q=(0,), k=(0,), v=(0,), n=(0,), out=(0,), u0=(0,), u1=(0,), d1=(0,)),
    f1=dict(q=(1,), k=(1,), v=(1,), u1=(1,)),
    f2=dict(q=(2,), k=(2,), v=(2,), out=(1,), u0=(1,), d1=(1,)),
    f3=dict(q=(3,), k=(3,), n=(1,), out=(2,), d0=(0,)),
    f4=dict(u1=(2,)),
    f5=dict(v=(3,), u0=(2,)),
    f6=dict(n=(2,), u1=(3,)),
    f7=dict(q=(4,), k=(4,), v=(4,)),
    pr1=dict(d1=(2,)),
    a=dict(d0=(1,)),
    m0=dict(out=(3,)),
    b0=dict(n=(3,), u0=(3,)),
    m2=dict(d0=(2,)),
    b2=dict(u1=(4,), d1=(3,)),
    b3=dict(out=(4,), u0=(4,), d0=(3,)),
    e0=dict(out=(5,), u1=(5,), d0=(4,), d1=(4,)),
    e1=dict(u0=(5,)),
    e2=dict(d0=(5,), d1=(5,)),
)
SCATTER_AT = dict(
    g0=dict(d0=(0,), d1=(0,)),
    g1=dict(u0=(0,), u1=(0,)),
    g2=dict(d0=(1,), u0=(1,)),
    g3=dict(d1=(1,), u1=(1,), out=(0,)),
    g4=dict(d0=(2,), u0=(2,), u1=(2,), out=(1,)),
    q0=dict(q=(0,)),
    q1=dict(u0=(3,), k=(0,)),
    q2=dict(v=(0,)),
    q3=dict(d0=(3,), d1=(2,), u1=(3,), out=(2,), q=(1,)),
    z0=dict(k=(1,), v=(1,)),
    z1=dict(d1=(3,), u0=(4,), u1=(4,), out=(3,), q=(2,), k=(2,), v=(2,)),
    z2=dict(d0=(4,), d1=(4,), out=(4,), q=(3,), k=(3,), v=(3,)),
    z3=dict(d0=(5,), d1=(5,), u0=(5,), u1=(5,), out=(5,), q=(4,), k=(4,), v=(4,)),
)
HEADS = ("q", "k", "v")


def x_lane(index):
    return index if isinstance(index, slice) else pl.ds(pl.multiple_of(index * 128, 128), 128)


class Refs:
    pass


class Layer:
    def __init__(self, sizes, rows, tokens_total, refs):
        self.r = refs
        self.sizes, self.rows, self.own, self.tokens_total = sizes, rows, rows // 4, tokens_total
        self.place = Place(sizes)
        at = self.place.at
        self.x, self.c, self.z, self.y = at["x"], at["c"], at["z"], at["y"]
        self.t = self.x * 2 + self.c
        self.shard = 512 // (sizes["z"] * sizes["y"])
        self.half = lanes((self.own, 128), HD)
        self.zero = jnp.zeros((self.own, 128), BF16)
        self.gathers = self.make_gathers()
        self.scatters = self.make_scatters()
        self.sent = []

    def make_gathers(self):
        r = self.r

        def qkv_view(i):
            return lambda w: r.qkv_all.at[i, w["z"], w["y"], w["r"], x_lane(w["x"])]

        def ff_view(start):
            return lambda w: r.ff_all.at[w["x"], w["c"], w["z"], w["y"], w["r"], pl.ds(start, 256)]

        views = {
            "q": qkv_view(0),
            "k": qkv_view(1),
            "v": qkv_view(2),
            "n": lambda w: r.counts.at[w["z"], w["y"], w["r"]],
            "out": lambda w: r.out_all.at[w["c"], w["z"], w["y"], w["r"], x_lane(w["x"])],
            "u0": ff_view(0),
            "u1": ff_view(256),
            "d0": ff_view(512),
            "d1": ff_view(768),
        }
        plans, base = {}, 0
        for name, order in GATHERS:
            rows = 16 if name == "n" else self.shard
            plans[name] = Gather(self.place, views[name], order, rows, r.send_w, r.recv_w, base)
            base += slots_of(self.sizes, order)
        return plans

    def make_scatters(self):
        r = self.r

        def ff_view(start):
            return lambda w: r.grad_ff.at[w["x"], w["c"], w["z"], w["y"], w["r"], pl.ds(start, 256)]

        def ff_kept(start):
            return lambda w: r.ff_work.at[w["x"], w["z"], w["y"], w["r"], pl.ds(start, 256)]

        def qkv_view(i):
            return lambda w: r.grad_qkv.at[i, w["z"], w["y"], w["r"], x_lane(w["x"])]

        views = {
            "u0": (ff_view(0), ff_kept(0), r.up_final.at[:, pl.ds(0, 256)]),
            "u1": (ff_view(256), ff_kept(256), r.up_final.at[:, pl.ds(256, 256)]),
            "d0": (ff_view(512), ff_kept(512), r.down_final.at[:, pl.ds(0, 256)]),
            "d1": (ff_view(768), ff_kept(768), r.down_final.at[:, pl.ds(256, 256)]),
            "out": (
                lambda w: r.grad_out.at[w["c"], w["z"], w["y"], w["r"], x_lane(w["x"])],
                lambda w: r.out_work.at[w["z"], w["y"], w["r"], x_lane(w["x"])],
                r.out_final,
            ),
        }
        for i, name in enumerate("qkv"):
            views[name] = (qkv_view(i), qkv_view(i), r.qkv_final.at[i])
        plans, base, used = {}, 0, 0
        for name, order, dims, width, lane_x in SCATTERS:
            view, kept, final = views[name]
            count = len(steps_of(self.sizes, order))
            landing = r.landing[used : used + count]
            plans[name] = Scatter(
                self.place, view, kept, order, dims, self.shard, 0, landing, final, r.send_g, r.recv_g, base
            )
            used += count
            base += slots_of(self.sizes, order)
        return plans

    def point(self, label):
        for plans, places in ((self.gathers, GATHER_AT), (self.scatters, SCATTER_AT)):
            for name, steps in places.get(label, {}).items():
                for step in steps:
                    plans[name].next(step)

    def within(self, index, label):
        if label in GATHER_AT or label in SCATTER_AT:

            @pl.when(index)
            def _():
                self.point(label)

    def local(self, index, src, dst):
        copy = pltpu.make_async_copy(src, dst, self.r.local_sem.at[index])
        copy.start()
        return copy

    def row_block(self, index):
        return pl.ds(pl.multiple_of(index * self.own, self.own), self.own)

    def run(self):
        self.front()
        self.attention()
        self.feed_forward()
        self.attention_back()
        self.end()

    def front(self):
        r, place, x, c, own = self.r, self.place, self.x, self.c, self.own
        met = place.meet()
        copies = [
            self.local(0, r.qkv_shard, r.qkv_all.at[:, self.z, self.y, :, x_lane(x)]),
            self.local(1, r.out_shard, r.out_all.at[c, self.z, self.y, :, x_lane(x)]),
            self.local(2, r.up_shard, r.ff_all.at[x, c, self.z, self.y, :, pl.ds(0, 512)]),
            self.local(3, r.down_shard, r.ff_all.at[x, c, self.z, self.y, :, pl.ds(512, 512)]),
        ]
        load_x = self.local(4, r.x_hbm, r.x_ref)
        load_tables = self.local(5, r.tables_hbm, r.tables)
        self.loads = [self.local(6, r.teacher_hbm, r.teacher), self.local(7, r.cotangent_hbm, r.cotangent)]
        total = r.lengths[0] + r.lengths[1]
        r.counts[self.z, self.y] = jnp.full((16, 128), total.astype(F32))
        for copy in copies:
            copy.wait()
        met()
        self.point("f0")
        load_x.wait()
        for s in range(2):
            center, scale = normalize(token_rows(r.x_ref, s, own))
            for j in range(4):
                lane = pl.ds(128 * j, 128)
                value = center[j] * scale * r.gain_1[:, lane] + r.shift_1[:, lane]
                r.own_normed[s, :, lane] = value.astype(BF16)
        mine = self.row_block(self.t)

        def tokens(index, ref, moves):
            return remote(ref, ref, r.send_n.at[index], r.recv_n.at[index], place.device(**moves))

        sent = [
            remote(r.own_normed.at[1 - x], r.normed_all.at[mine], r.send_n.at[0], r.recv_n.at[0], place.device(x=1)),
            remote(r.own_normed.at[x], r.normed_all.at[mine], r.send_n.at[1], r.recv_n.at[1], place.device(c=1)),
        ]
        for copy in sent:
            copy.start()
        keep = self.local(0, r.own_normed.at[x], r.normed_all.at[mine])
        for label in ("f1", "f2", "f3"):
            self.point(label)
        far = r.normed_all.at[self.row_block((1 - x) * 2 + c)]
        tokens(0, far, {"x": 1}).wait_recv()
        sent.append(tokens(2, far, {"c": 1}))
        sent[-1].start()
        self.point("f4")
        self.point("f5")
        keep.wait()
        tokens(1, r.normed_all.at[self.row_block(x * 2 + 1 - c)], {"c": 1}).wait_recv()
        self.point("f6")
        tokens(2, r.normed_all.at[self.row_block((1 - x) * 2 + 1 - c)], {"c": 1}).wait_recv()
        self.point("f7")
        load_tables.wait()
        self.sent += sent

        w_qkv = [r.qkv_all[i].reshape(-1, 256) for i in range(3)]

        def project(index, carry):
            here = pl.ds(pl.multiple_of(index * own, own), own)
            normed = r.normed_all[here, :]
            cos, sin_a, sin_b = (r.tables[i, here, :] for i in range(3))
            for i, ref in ((0, r.q_all), (1, r.k_all), (2, r.v_all)):
                value = dot(normed, w_qkv[i])
                for pair in range(2):
                    lane = pl.ds(128 * pair, 128)
                    part = value[:, 128 * pair : 128 * pair + 128]
                    if i < 2:
                        part = rope(part, cos, sin_a, sin_b)
                    if i == 0:
                        part = part.astype(BF16) * jnp.asarray(HD**-0.5, BF16)
                    ref[here, lane] = part.astype(BF16)
            self.within(index == 1, "pr1")
            return carry

        lax.fori_loop(0, 4, project, 0)
        self.point("a")

    def hand(self, qb, act):
        r, t = self.r, self.t
        source, target = r.own_attended.at[pl.ds(qb * self.own, self.own)], r.attended.at[self.c, self.x]
        device = (lax.axis_index("dp"), jnp.asarray(qb, jnp.int32))

        @pl.when(t != qb)
        def _():
            copy = remote(source, target, r.send_a.at[qb], r.recv_a.at[t], device)
            copy.start() if act == "start" else copy.wait_send()

        if act == "start":

            @pl.when(t == qb)
            def _():
                pltpu.make_async_copy(source, target, r.recv_a.at[t]).start()

    def attention(self):
        r, own, half, zero = self.r, self.own, self.half, self.zero
        length = r.lengths[self.x]
        for qb in range(4):
            here = pl.ds(qb * own, own)
            keys = (qb + 1) * own
            key_pos = lax.broadcasted_iota(jnp.int32, (own, keys), 1)
            query_pos = lax.broadcasted_iota(jnp.int32, (own, keys), 0) + qb * own
            allowed = key_pos <= query_pos
            if qb > 1:
                allowed = allowed & (key_pos < length)

            def attend(pair, carry, qb=qb, here=here, keys=keys, allowed=allowed):
                lane = pl.ds(pl.multiple_of(pair * 128, 128), 128)
                queries = r.q_all[here, lane]
                k_part = r.k_all[pl.ds(0, keys), lane]
                v_part = r.v_all[pl.ds(0, keys), lane]
                mixed = []
                for head in range(2):
                    masked = jnp.where(half, queries, zero) if head == 0 else jnp.where(half, zero, queries)
                    scores = jnp.where(allowed, dot(masked, k_part, NT), -1e30)
                    highest = jnp.max(scores, -1, keepdims=True)
                    expd = jnp.exp(scores - highest)
                    denom = jnp.sum(expd, -1, keepdims=True)
                    probs = (expd * (1.0 / denom)).astype(BF16)
                    mixed.append(dot(probs, v_part))
                    wide = jnp.broadcast_to(highest + jnp.log(denom), (own, 128))
                    r.lse[pair * 2 + head, :, here] = jnp.transpose(wide)[:8]
                r.own_attended[here, lane] = jnp.where(half, mixed[0], mixed[1]).astype(BF16)
                self.within(pair == 0, "m%d" % qb)
                return carry

            lax.fori_loop(0, 2, attend, 0)
            self.hand(qb, "start")
            self.point("b%d" % qb)
        for pair in range(2):
            r.k_t[pair] = jnp.transpose(r.k_all[:, pl.ds(128 * pair, 128)])
        for k in range(2):
            for s in range(2):
                came = r.attended.at[k, s]
                remote(came, came, r.send_a.at[0], r.recv_a.at[s * 2 + k], self.place.device(x=1)).wait_recv()

    def feed_forward(self):
        r, own = self.r, self.own
        self.point("e0")
        count = jnp.sum(r.counts[...], axis=(0, 1))[0:1]
        factor = self.tokens_total / count
        weights = [r.out_all[k].reshape(512, 256) for k in range(2)]
        valid = []
        for s in range(2):
            rows = pl.ds(s * own, own)
            attn = dot(r.attended[0, s], weights[0], NT) + dot(r.attended[1, s], weights[1], NT)
            parts = token_rows(r.x_ref, s, own)
            for j in range(4):
                r.middle[rows, pl.ds(128 * j, 128)] = parts[j] + attn[:, 128 * j : 128 * j + 128]
            position = self.t * own + lax.broadcasted_iota(jnp.int32, (own, 128), 0)
            valid.append((position < r.lengths[s]).astype(F32))
        value = r.middle[...]
        mean = jnp.mean(value, -1, keepdims=True)
        center = value - mean
        scale = lax.rsqrt(jnp.mean(center * center, -1, keepdims=True) + 1e-05)
        normed = (center * scale * r.gain_2[...] + r.shift_2[...]).astype(BF16)
        normed_t = jnp.transpose(normed)

        def weight(t, start):
            return r.ff_all[t // 2, t % 2, :, :, :, pl.ds(start, 512)].reshape(512, 512)

        self.point("e1")

        def up(t, carry):
            act, slope = gelu_parts(dot(normed, weight(t, 0)))
            r.slope[t] = slope
            r.hidden[t] = act.astype(BF16)
            return carry

        lax.fori_loop(0, 4, up, 0)
        self.point("e2")
        r.total_sum[...] = jnp.zeros_like(r.total_sum)

        def down(t, carry):
            r.total_sum[...] += dot(r.hidden[t], weight(t, 512), NT)
            return carry

        lax.fori_loop(0, 4, down, 0)
        self.point("e3")
        for copy in self.loads:
            copy.wait()
        square = jnp.zeros((own, 128), F32)
        for s in range(2):
            rows = pl.ds(s * own, own)
            want = token_rows(r.teacher, s, own)
            pull = token_rows(r.cotangent, s, own)
            for j in range(4):
                lane = pl.ds(128 * j, 128)
                out = r.middle[rows, lane] + r.total_sum[rows, lane]
                r.output[pl.ds(2 * j + s, own, stride=8), :] = out
                differ = out - want[j]
                square = square + valid[s] * differ * differ
                r.seed[rows, lane] = factor * valid[s] * (pull[j] + differ)
        self.store = self.local(6, r.output, r.output_hbm)
        grad_f = r.seed[...].astype(BF16)
        grad_f_t = jnp.transpose(grad_f)
        r.total_sum[...] = jnp.zeros_like(r.total_sum)

        def put(t, start, value):
            value = value.astype(BF16).reshape(self.sizes["z"], self.sizes["y"], self.shard, 512)
            r.grad_ff[t // 2, t % 2, :, :, :, pl.ds(start, 512)] = value

        def back_down(t, carry):
            put(t, 512, dot(grad_f_t, r.hidden[t]))
            return carry

        lax.fori_loop(0, 4, back_down, 0)
        self.point("g0")

        def back_up(t, carry):
            grad_before = (r.slope[t] * dot(grad_f, weight(t, 512))).astype(BF16)
            put(t, 0, dot(normed_t, grad_before))
            r.total_sum[...] += dot(grad_before, weight(t, 0), NT)
            return carry

        lax.fori_loop(0, 4, back_up, 0)
        self.point("g1")
        grad_normed = r.total_sum[...]
        unit = (r.middle[...] - mean) * scale
        r.stat_send[0] = jnp.zeros_like(r.stat_send[0])
        r.stat_send[0, 0:1, 0:128] = jnp.sum(square, 0, keepdims=True)
        r.stat_send[0, 1:2] = jnp.sum(grad_normed * unit, 0, keepdims=True)
        r.stat_send[0, 2:3] = jnp.sum(grad_normed, 0, keepdims=True)
        scaled = grad_normed * r.gain_2[...]
        inner = jnp.mean(scaled * unit, -1, keepdims=True)
        grad = r.seed[...] + scale * (scaled - jnp.mean(scaled, -1, keepdims=True) - unit * inner)
        r.grad_middle[...] = grad
        branch = grad.astype(BF16)
        for k in range(2):
            grads = dot(branch, weights[k]).astype(BF16)
            for s in range(2):
                r.grad_attended[k, s] = grads[s * own : s * own + own]
        self.send_attended_back()
        self.point("g2")
        branch_t = jnp.transpose(branch)
        for k in range(2):
            value = dot(branch_t[:, :own], r.attended[k, 0]) + dot(branch_t[:, own:], r.attended[k, 1])
            r.grad_out[k] = value.astype(BF16).reshape(self.sizes["z"], self.sizes["y"], self.shard, 256)
        self.point("g3")

    def send_attended_back(self):
        r, at = self.r, self.place.at
        mine = r.g_all.at[self.row_block(self.t)]
        for index, moves in enumerate(({"x": 1}, {"x": 1, "c": 1}, {"c": 1})):
            to = dict(at)
            for axis in moves:
                to[axis] = 1 - at[axis]
            source = r.grad_attended.at[to["c"], to["x"]]
            copy = remote(source, mine, r.send_b.at[index], r.recv_b.at[self.t], self.place.device(**moves))
            copy.start()
            self.sent.append(copy)
        pltpu.make_async_copy(r.grad_attended.at[self.c, self.x], mine, r.recv_b.at[self.t]).start()

    def to_core(self, qb, act):
        r, i = self.r, qb // 2

        @pl.when(self.c != qb % 2)
        def _():
            source = r.grad_n.at[pl.ds(qb * self.own, self.own)]
            copy = remote(source, r.from_core.at[i], r.send_n.at[3 + i], r.recv_n.at[3 + i], self.place.device(c=1))
            copy.start() if act == "start" else copy.wait_send()

    def core_arrived(self, index):
        r = self.r
        slot = r.from_core.at[index]
        remote(slot, slot, r.send_n.at[3], r.recv_n.at[3 + index], self.place.device(c=1)).wait_recv()

    def cross(self):
        r = self.r
        return remote(r.to_x, r.from_x, r.send_n.at[5], r.recv_n.at[5], self.place.device(x=1))

    def to_chip(self, qb):
        r = self.r

        @pl.when((self.c == qb % 2) & (self.x != qb // 2))
        def _():
            self.core_arrived(qb // 2)
            r.to_x[...] = (r.grad_n[pl.ds(qb * self.own, self.own), :] + r.from_core[qb // 2]).astype(BF16)
            self.cross().start()

    def attention_back(self):
        r, own, half, zero = self.r, self.own, self.half, self.zero
        normed_t = jnp.transpose(r.normed_all[...])
        length = r.lengths[self.x]
        upper = lax.broadcasted_iota(jnp.int32, (128, own), 0) < HD
        w_qkv = [r.qkv_all[i].reshape(512, 256) for i in range(3)]
        self.point("g4")
        for qb in range(3, -1, -1):
            here = pl.ds(qb * own, own)
            keys = (qb + 1) * own
            seen = pl.ds(0, keys)
            key_pos = lax.broadcasted_iota(jnp.int32, (keys, own), 0)
            query_pos = lax.broadcasted_iota(jnp.int32, (keys, own), 1) + qb * own
            allowed = key_pos <= query_pos
            if qb > 1:
                allowed = allowed & (key_pos < length)
            came = r.g_all.at[here]
            remote(came, came, r.send_b.at[0], r.recv_b.at[qb], self.place.device(x=1)).wait_recv()

            def attend(pair, carry, qb=qb, here=here, seen=seen, allowed=allowed):
                lane = pl.ds(pl.multiple_of(pair * 128, 128), 128)
                queries = r.q_all[here, lane]
                grads = r.g_all[here, lane]
                k_part = r.k_all[seen, lane]
                v_part = r.v_all[seen, lane]
                dq = []
                for head in range(2):
                    if head == 0:
                        q_m, g_m = jnp.where(half, queries, zero), jnp.where(half, grads, zero)
                    else:
                        q_m, g_m = jnp.where(half, zero, queries), jnp.where(half, zero, grads)
                    scores = dot(k_part, q_m, NT)
                    probs = jnp.where(allowed, jnp.exp(scores - r.lse[pair * 2 + head, 0:1, here]), 0.0)
                    grad_probs = dot(v_part, g_m, NT)
                    inner = jnp.sum(probs * grad_probs, 0, keepdims=True)
                    grad_raw = (probs * (grad_probs - inner)).astype(BF16)
                    add_k = dot(grad_raw, q_m)
                    add_v = dot(probs.astype(BF16), g_m)
                    if qb == 3 and head == 0:
                        r.grad_k[seen, lane] = add_k
                        r.grad_v[seen, lane] = add_v
                    else:
                        r.grad_k[seen, lane] += add_k
                        r.grad_v[seen, lane] += add_v
                    dq.append(dot(r.k_t[pair, :, seen], grad_raw))
                r.grad_q[here, lane] = jnp.transpose(jnp.where(upper, dq[0], dq[1])) * HD**-0.5
                self.within(pair == 0, "n%d" % qb)
                return carry

            lax.fori_loop(0, 2, attend, 0)

            cos, sin_a, sin_b = (r.tables[i, here, :] for i in range(3))
            total = jnp.zeros((own, 512), F32)
            for i, ref in ((0, r.grad_q), (1, r.grad_k), (2, r.grad_v)):
                for pair in range(2):
                    lane = pl.ds(128 * pair, 128)
                    part = ref[here, lane]
                    if i < 2:
                        part = rope_back(part, cos, sin_a, sin_b)
                    r.grad_proj[i, here, lane] = part.astype(BF16)
                total = total + dot(r.grad_proj[i, here, :], w_qkv[i], NT)
            r.grad_n[here, :] = total
            self.to_core(qb, "start")
            if qb < 3:
                self.to_chip(qb + 1)
            self.point("t%d" % qb)
        for i, name in enumerate(HEADS):
            value = dot(normed_t, r.grad_proj[i]).astype(BF16)
            r.grad_qkv[i] = value.reshape(self.sizes["z"], self.sizes["y"], self.shard, 256)
            if i == 1:
                self.to_chip(0)
            self.point("q%d" % i)

    def end(self):
        r, own, x = self.r, self.own, self.x
        self.point("q3")
        self.core_arrived(x)
        self.cross().wait_recv()
        self.point("z0")
        grad_gain = [jnp.zeros((1, 128), F32)] * 4
        grad_shift = [jnp.zeros((1, 128), F32)] * 4
        for s in range(2):
            center, scale = normalize(token_rows(r.x_ref, s, own))
            near = r.grad_n[self.row_block(self.t), :] + r.from_core[x]
            chosen = jnp.where(x == s, near, r.from_x[...].astype(F32))
            grads = [chosen[:, 128 * j : 128 * j + 128] for j in range(4)]
            units = [part * scale for part in center]
            scaled = [grads[j] * r.gain_1[:, pl.ds(128 * j, 128)] for j in range(4)]
            mean = row_mean(scaled)
            inner = row_mean([scaled[j] * units[j] for j in range(4)])
            for j in range(4):
                part = r.grad_middle[pl.ds(s * own, own), pl.ds(128 * j, 128)]
                grad = part + scale * (scaled[j] - mean - units[j] * inner)
                r.grad_inputs[pl.ds(2 * j + s, own, stride=8), :] = grad
                grad_gain[j] = grad_gain[j] + jnp.sum(grads[j] * units[j], 0, keepdims=True)
                grad_shift[j] = grad_shift[j] + jnp.sum(grads[j], 0, keepdims=True)
        for j in range(4):
            r.stat_send[0, 3:4, 128 * j : 128 * j + 128] = grad_gain[j]
            r.stat_send[0, 4:5, 128 * j : 128 * j + 128] = grad_shift[j]
        slot = 0
        for phase, peers in enumerate((self.place.group(), self.place.across())):
            came = []
            for peer in peers:
                came.append(
                    remote(r.stat_send.at[phase], r.stat_land.at[slot], r.send_s.at[slot], r.recv_s.at[slot], peer)
                )
                came[-1].start()
                slot += 1
            self.point("z%d" % (phase + 1))
            total = r.stat_send[phase]
            for index, copy in enumerate(came):
                copy.wait_recv()
                total = total + r.stat_land[slot - len(came) + index]
            if phase == 0:
                r.stat_send[1] = total
            else:
                r.stats_final[...] = total
            self.sent += came
        self.point("z3")
        for plan in list(self.gathers.values()) + list(self.scatters.values()):
            plan.finish()
        for copy in self.sent + [self.cross()]:
            copy.wait_send()
        for qb in range(4):
            self.hand(qb, "finish")
            self.to_core(qb, "finish")
        self.store.wait()


def whole(sizes, rows, tokens_total, operands):
    zs, ys = sizes["z"], sizes["y"]
    shard = 512 // (zs * ys)
    own = rows // 4
    wide = own * 8
    inputs = dict(
        lengths=0, gain_1=0, shift_1=0, gain_2=0, shift_2=0, x_hbm=0,
        teacher_hbm=0, cotangent_hbm=0, tables_hbm=0, qkv_shard=0, out_shard=0, up_shard=0, down_shard=0,
    )
    outputs = dict(
        output_hbm=(wide, 128),
        grad_inputs=(wide, 128),
        up_final=(shard, 512),
        down_final=(shard, 512),
        out_final=(shard, 128),
        qkv_final=(3, shard, 128),
        stats_final=(8, 512),
        counts=(zs, ys, 16, 128),
    )
    scratch = dict(
        x_ref=((wide, 128), F32),
        teacher=((wide, 128), F32),
        cotangent=((wide, 128), F32),
        output=((wide, 128), F32),
        tables=((3, rows, 128), F32),
        ff_all=((2, 2, zs, ys, shard, 1024), BF16),
        out_all=((2, zs, ys, shard, 256), BF16),
        qkv_all=((3, zs, ys, shard, 256), BF16),
        own_normed=((2, own, 512), BF16),
        normed_all=((rows, 512), BF16),
        q_all=((rows, 256), BF16),
        k_all=((rows, 256), BF16),
        v_all=((rows, 256), BF16),
        k_t=((2, 128, rows), BF16),
        lse=((4, 8, rows), F32),
        own_attended=((rows, 256), BF16),
        attended=((2, 2, own, 256), BF16),
        middle=((2 * own, 512), F32),
        seed=((2 * own, 512), F32),
        slope=((4, 2 * own, 512), F32),
        hidden=((4, 2 * own, 512), BF16),
        total_sum=((2 * own, 512), F32),
        grad_middle=((2 * own, 512), F32),
        grad_attended=((2, 2, own, 256), BF16),
        grad_ff=((2, 2, zs, ys, shard, 1024), BF16),
        grad_out=((2, zs, ys, shard, 256), BF16),
        g_all=((rows, 256), BF16),
        grad_q=((rows, 256), F32),
        grad_k=((rows, 256), F32),
        grad_v=((rows, 256), F32),
        grad_proj=((3, rows, 256), BF16),
        grad_qkv=((3, zs, ys, shard, 256), BF16),
        grad_n=((rows, 512), F32),
        ff_work=((2, zs, ys, shard, 1024), BF16),
        out_work=((zs, ys, shard, 256), BF16),
        from_core=((2, own, 512), F32),
        to_x=((own, 512), BF16),
        from_x=((own, 512), BF16),
        stat_send=((2, 8, 512), F32),
        stat_land=((zs * ys + 2, 8, 512), F32),
    )
    gathered = sum(slots_of(sizes, order) for _, order in GATHERS)
    scattered = sum(slots_of(sizes, item[1]) for item in SCATTERS)
    sems = dict(local_sem=8, send_w=gathered, recv_w=gathered, send_g=scattered, recv_g=scattered)
    sems |= dict(send_n=6, recv_n=6, send_a=4, recv_a=4, send_b=3, recv_b=4)
    sems |= dict(send_s=zs * ys + 2, recv_s=zs * ys + 2)
    lands = []
    for _, order, dims, width, lane_x in SCATTERS:
        lands += landing_shapes(sizes, order, dims, shard, width, lane_x=lane_x)

    def kernel(*refs):
        refs = list(refs)
        out = Refs()
        for name in list(inputs) + list(outputs) + list(scratch) + list(sems):
            setattr(out, name, refs.pop(0))
        out.landing = refs
        Layer(sizes, rows, tokens_total, out).run()

    any_spec = pl.BlockSpec(memory_space=pl.ANY)
    vmem = pl.BlockSpec(memory_space=pltpu.VMEM)
    return pl.pallas_call(
        kernel,
        out_shape=[jax.ShapeDtypeStruct(shape, F32) for shape in outputs.values()],
        in_specs=[pl.BlockSpec(memory_space=pltpu.SMEM)] + [vmem] * 4 + [any_spec] * 8,
        out_specs=[any_spec] + [vmem] * (len(outputs) - 1),
        scratch_shapes=[pltpu.VMEM(*shape) for shape in scratch.values()]
        + [pltpu.SemaphoreType.DMA((count,)) for count in sems.values()]
        + [pltpu.VMEM(shape, BF16) for shape in lands],
        name="whole",
        compiler_params=pltpu.CompilerParams(
            collective_id=0, has_side_effects=True, vmem_limit_bytes=VMEM_LIMIT
        ),
    )(*operands)


def last_kernel(features, counts, output, grad_inputs, up, down, out, qkv, sums, *outs):
    for source, target in zip((output, grad_inputs, up, down, out, qkv), outs[:6]):
        target[...] = source[...]
    for target, row in zip(outs[6:10], (3, 4, 1, 2)):
        target[...] = sums[row : row + 1]
    total = jnp.sum(counts[...], axis=0)[0:1, 0:1]
    outs[10][...] = jnp.sum(sums[0:1, 0:128], -1, keepdims=True) / (total * features)


def last(features, counts, output, grad_inputs, up, down, out, qkv, sums):
    vmem = pl.BlockSpec(memory_space=pltpu.VMEM)
    shapes = [value.shape for value in (output, grad_inputs, up, down, out, qkv)] + [(1, features)] * 4 + [(1, 1)]
    return pl.pallas_call(
        lambda *refs: last_kernel(features, *refs),
        out_shape=[jax.ShapeDtypeStruct(shape, F32) for shape in shapes],
        in_specs=[vmem] * 8,
        out_specs=[vmem] * len(shapes),
        name="last",
        compiler_params=pltpu.CompilerParams(vmem_limit_bytes=VMEM_LIMIT),
    )(counts, output, grad_inputs, up, down, out, qkv, sums)


def solution(mesh):
    dp, tensor = mesh.shape["dp"], mesh.shape["tensor"]
    sizes = {"z": dp // 2, "y": 2, "x": tensor // 2, "c": 2}

    def shards(
        inputs, qkv_weight, out_weight, up_weight, down_weight, gain_one, shift_one, gain_two, shift_two, lengths,
        teacher, cotangent,
    ):
        own, sequences, width = inputs.shape
        rows = own * tensor

        def packed(value):
            view = value.reshape(own, sequences, width // 128, 128).transpose(0, 2, 1, 3)
            return view.reshape(own * sequences * (width // 128), 128)

        def unpacked(value):
            view = value.reshape(own, width // 128, sequences, 128).transpose(0, 2, 1, 3)
            return view.reshape(own, sequences, width)

        operands = (
            lengths, gain_one[None], shift_one[None], gain_two[None], shift_two[None], packed(inputs), packed(teacher),
            packed(cotangent), rope_tables(rows), qkv_weight, out_weight.T, up_weight, down_weight.T,
        )
        *parts, sums, counts = whole(sizes, rows, float(rows * sequences * dp), operands)
        output, grad_inputs, up, down, out, qkv, gain_1, shift_1, gain_2, shift_2, loss = last(
            width, counts.reshape(dp, 16, 128), *parts, sums
        )
        return (
            unpacked(output), loss.reshape(()), unpacked(grad_inputs), qkv, out.T, up, down.T, gain_1.reshape(width),
            shift_1.reshape(width), gain_2.reshape(width), shift_2.reshape(width),
        )

    tokens, rows_dp, cols_dp = P("tensor", "dp", None), P("dp", "tensor"), P("tensor", "dp")
    heads = P(None, "dp", "tensor")
    return jax.shard_map(
        shards,
        mesh=mesh,
        in_specs=(tokens, heads, cols_dp, rows_dp, cols_dp, P(), P(), P(), P(), P("dp"), tokens, tokens),
        out_specs=(tokens, P(), tokens, heads, cols_dp, rows_dp, cols_dp, P(), P(), P(), P()),
        check_vma=False,
    )
```

time: 853 us -> 117 us (0.14)
  waiting for transfers between devices: 406 us -> 0 us
  blocking collectives: 189 us -> 0 us
  matrix products: 154 us -> 0 us
  Pallas kernels: 0 us -> 116 us
  other arithmetic: 55.5 us -> 0 us
  local copies, waits for them, and re-layouts: 24.8 us -> 0 us
  between operations: 19.7 us -> 0.83 us
    reduce_scatter x7 -> x0, waiting for transfers between devices: 308 us -> none  [the longest x1 67.1 us: shards(): lax.psum_scatter(grad_down_weight, 'dp', scatter_dimension=1, tiled=True)]
    dot_general x24 -> x0, matrix products: 154 us -> none  [the longest x2 42.1 us: shards(): jnp.einsum('shqk,kshe->qshe', grad_raw, keys_all, preferred_element_type=...]
    all_gather x4 -> x0, blocking collectives: 127 us -> none  [the longest x1 32.3 us: shards(): lax.all_gather(out_weight, 'dp', axis=1, tiled=True)]
    pallas_call x0 -> x2, Pallas kernels: none -> 116 us  [the longest x1 113 us: whole(): pl.pallas_call(kernel, out_shape=[jax.ShapeDtypeStruct(shape, F32) for sh...]
    psum x2 -> x0, blocking collectives: 62 us -> none  [the longest x1 40 us: shards(): lax.psum((square_part, grad_gain_one, grad_shift_one, grad_gain_two, grad...]
    unnamed x13 -> x0, waiting for transfers between devices: 56.6 us -> none
    all_gather x4 -> x0, waiting for transfers between devices: 41.7 us -> none  [the longest x1 22.7 us: shards(): lax.all_gather(seed.astype(jnp.bfloat16), 'tensor', axis=0, tiled=True)]
    reduce_sum x11 -> x0, other arithmetic: 20.1 us -> none  [the longest x3 5.95 us: norm_rows(): return center * lax.rsqrt(spread + 1e-05) * gain + shift]
  transfers between devices with their start and end apart: 12 -> 0, of which waited for: 10 -> 0; matrix products, arithmetic and copies ran while one was open for 4% -> 0% of each run, Pallas kernels for 0% -> 0%
where the time goes in v3:
time: 117 us
  Pallas kernels  116 us (99%)
    pallas_call x1, Pallas kernels, whole(): pl.pallas_call(kernel, out_shape=[jax.ShapeDtypeStruct(shape, F32) for sh...  113 us
    pallas_call x1, Pallas kernels, last(): pl.pallas_call(lambda *refs: last_kernel(features, *refs), out_shape=[jax...  3.32 us

profile of v3, /device:TPU:0, one launch (start us, length us, event | category | flops | bytes accessed | tf_op | source)
XLA Modules:
  0.0 117.0 jit_solution(15408501894244579612)
XLA Ops:
  0.6 112.8 %whole.1 = (f32[2048,128]{1,0:T(8,128)}, f32[2048,128]{1,0:T(8,128)}, f32[64,512]{1,0:T(8,128)}, f32[64,512]{1,0:T(8,128)}, f32[64,128]{1,0:T(8,128)}, /*index=5...) custom-call(s32[2]{0:T(128)} %refs_0_.1, f32[1,512]{1,0:T(1,128)} %bitcast.45, f32[1,512]{1,0:T(1,128)} %bitcast.46, ...), custom_call_target="tpu_custom_call" | custom-call | tf_op jit(solution)/shard_map/whole/pallas_call | solution.py:953
  113.5 3.3 %last.1 = (f32[2048,128]{1,0:T(8,128)}, f32[2048,128]{1,0:T(8,128)}, f32[64,512]{1,0:T(8,128)}, f32[64,512]{1,0:T(8,128)}, f32[64,128]{1,0:T(8,128)}, /*index=5*...) custom-call(f32[8,16,128]{2,1,0:T(8,128)} %bitcast.43, ...), custom_call_target="tpu_custom_call" | custom-call | tf_op jit(solution)/shard_map/last/pallas_call | solution.py:980

commit v4 on v3

--- a/solution.py
+++ b/solution.py
@@ -69,12 +69,19 @@
 def steps_of(sizes, order):
     out = []
     for axis in order:
-        out += ["z1", "z2"] if axis == "z" and sizes["z"] == 4 else [axis]
+        if axis in "zZ":
+            out += ["z1", "z2"] if axis == "z" and sizes["z"] == 4 else ["Z"]
+        else:
+            out.append(axis)
     return out
 
 
+def axis_of(step):
+    return step[0].lower()
+
+
 def slots_of(sizes, order):
-    return sum(2 if step in ("z1", "z2") else sizes[step] - 1 for step in steps_of(sizes, order))
+    return sum(2 if step in ("z1", "z2") else sizes[axis_of(step)] - 1 for step in steps_of(sizes, order))
 
 
 class Gather:
@@ -83,11 +90,12 @@
         self.send, self.recv, self.base = send, recv, base
         self.low, self.high = pl.ds(0, rows // 2), pl.ds(rows // 2, rows // 2)
         self.steps = steps_of(place.sizes, order)
+        self.order = order.lower()
 
     def part(self, step, **changed):
         where = dict(self.place.at)
         where["r"] = slice(None)
-        for axis in self.order[: self.order.index(self.steps[step][0])]:
+        for axis in self.order[: self.order.index(axis_of(self.steps[step]))]:
             where[axis] = slice(None)
         where.update(changed)
         return self.view(where)
@@ -102,6 +110,7 @@
                 far = self.part(step, z=moved("z", 2), r=rows)
                 out.append((self.part(step, z=moved("z", -d), r=rows), far, {"z": d}))
             return out
+        name = axis_of(name)
         size = self.place.sizes[name]
         return [
             (self.part(step), self.part(step, **{name: moved(name, -d)}), {name: d}) for d in range(1, size)
@@ -183,9 +192,10 @@
         self.send, self.recv, self.base = send, recv, base
         self.low, self.high = pl.ds(0, rows // 2), pl.ds(rows // 2, rows // 2)
         self.steps = steps_of(place.sizes, order)
+        self.order = order.lower()
 
     def done(self, step):
-        return self.order[: self.order.index(self.steps[step][0])]
+        return self.order[: self.order.index(axis_of(self.steps[step]))]
 
     def part(self, step, kept=False, **changed):
         where = dict(self.place.at)
@@ -202,13 +212,14 @@
             return [({"z": moved("z", 2), "r": rows}, {"z": d}) for d, rows in ((1, self.low), (-1, self.high))]
         if name == "z2":
             return [({"z": moved("z", d)}, {"z": d}) for d in (1, -1)]
+        name = axis_of(name)
         return [({name: moved(name, d)}, {name: d}) for d in range(1, self.place.sizes[name])]
 
     def sums(self, step):
         name, moved = self.steps[step], self.place.moved
         if name == "z1":
             return [({"z": moved("z", 1), "r": self.low}, [0]), ({"z": moved("z", -1), "r": self.high}, [1])]
-        return [({name[0]: self.place.at[name[0]]}, list(range(len(self.sends(step)))))]
+        return [({axis_of(name): self.place.at[axis_of(name)]}, list(range(len(self.sends(step)))))]
 
     def made(self, step):
         slot = self.base
@@ -230,7 +241,7 @@
     def arrive(self, step):
         for copy in self.made(step):
             copy.wait_recv()
-        axis = self.steps[step][0]
+        axis = axis_of(self.steps[step])
         rest = [a for a in self.dims if a in self.order and a not in self.done(step) and a != axis]
         sizes = [self.place.sizes[a] for a in rest]
         landing = self.landing[step]
@@ -271,10 +282,10 @@
 
 
 def landing_shapes(sizes, order, dims, rows, width, lead=(), lane_x=False):
-    left = list(order)
+    left = list(order.lower())
     shapes = []
     for step in steps_of(sizes, order):
-        axis = step[0]
+        axis = axis_of(step)
         if step != "z2" and axis in left:
             left.remove(axis)
         count = 2 if step in ("z1", "z2") else sizes[axis] - 1
@@ -291,60 +302,63 @@
 
 
 GATHERS = (
-    ("q", "zyx"),
-    ("k", "xzy"),
-    ("v", "xyz"),
+    ("q", "Zyx"),
+    ("k", "xyz"),
+    ("v", "Zxy"),
     ("n", "zy"),
-    ("out", "zyxc"),
-    ("u0", "xzyc"),
-    ("u1", "yzxc"),
-    ("d0", "xyzc"),
+    ("out", "xyZc"),
+    ("u0", "Zxyc"),
+    ("u1", "Zxyc"),
+    ("d0", "Zxyc"),
     ("d1", "xyzc"),
 )
 SCATTERS = (
-    ("d0", "czyx", "xczy", 256, False),
-    ("d1", "cxzy", "xczy", 256, False),
-    ("u0", "czxy", "xczy", 256, False),
-    ("u1", "czyx", "xczy", 256, False),
-    ("out", "cyzx", "czy", 128, True),
-    ("q", "zyx", "zy", 128, True),
-    ("k", "zxy", "zy", 128, True),
-    ("v", "yxz", "zy", 128, True),
+    ("d0", "cZyx", "xczy", 256, False),
+    ("d1", "cyZx", "xczy", 256, False),
+    ("u0", "cxyZ", "xczy", 256, False),
+    ("u1", "cyZx", "xczy", 256, False),
+    ("out", "cxZy", "czy", 128, True),
+    ("q", "yZx", "zy", 128, True),
+    ("k", "yxZ", "zy", 128, True),
+    ("v", "yZx", "zy", 128, True),
 )
 GATHER_AT = dict(
-    f0=dict(q=(0,), k=(0,), v=(0,), n=(0,), out=(0,), u0=(0,), u1=(0,), d1=(0,)),
-    f1=dict(q=(1,), k=(1,), v=(1,), u1=(1,)),
-    f2=dict(q=(2,), k=(2,), v=(2,), out=(1,), u0=(1,), d1=(1,)),
-    f3=dict(q=(3,), k=(3,), n=(1,), out=(2,), d0=(0,)),
-    f4=dict(u1=(2,)),
-    f5=dict(v=(3,), u0=(2,)),
-    f6=dict(n=(2,), u1=(3,)),
-    f7=dict(q=(4,), k=(4,), v=(4,)),
-    pr1=dict(d1=(2,)),
-    a=dict(d0=(1,)),
-    m0=dict(out=(3,)),
-    b0=dict(n=(3,), u0=(3,)),
-    m2=dict(d0=(2,)),
-    b2=dict(u1=(4,), d1=(3,)),
-    b3=dict(out=(4,), u0=(4,), d0=(3,)),
-    e0=dict(out=(5,), u1=(5,), d0=(4,), d1=(4,)),
-    e1=dict(u0=(5,)),
-    e2=dict(d0=(5,), d1=(5,)),
+    f0=dict(q=(0,), k=(0,), v=(0,), out=(0,), u1=(0,), d1=(0,)),
+    f1=dict(k=(1, 2,), n=(0,), u0=(0,)),
+    f2=dict(q=(1,), v=(1,), u1=(1,), d1=(1,)),
+    f3=dict(v=(2,)),
+    f4=dict(q=(2,), k=(3,), out=(1,), d0=(0,)),
+    f5=dict(n=(1,), u1=(2,)),
+    f6=dict(u0=(1,), d1=(2,)),
+    f7=dict(q=(3,), k=(4,), v=(3,)),
+    m0=dict(n=(2,), out=(2,), d0=(1,)),
+    b0=dict(u0=(2,)),
+    m2=dict(u1=(3,)),
+    b2=dict(d0=(2,)),
+    m3=dict(d1=(3,)),
+    b3=dict(out=(3,), u0=(3,)),
+    e0=dict(n=(3,), out=(4,)),
+    e1=dict(u0=(4,), u1=(4,), d0=(3,), d1=(4,)),
+    e2=dict(d0=(4,), d1=(5,)),
 )
 SCATTER_AT = dict(
-    g0=dict(d0=(0,), d1=(0,)),
+    g0=dict(d0=(0,)),
     g1=dict(u0=(0,), u1=(0,)),
-    g2=dict(d0=(1,), u0=(1,)),
-    g3=dict(d1=(1,), u1=(1,), out=(0,)),
-    g4=dict(d0=(2,), u0=(2,), u1=(2,), out=(1,)),
+    g2=dict(d0=(1,), u0=(1,), u1=(1,)),
+    g3=dict(d1=(0, 1,)),
+    g4=dict(out=(0, 1,)),
+    n3=dict(u1=(2,)),
+    n2=dict(u0=(2,)),
+    t2=dict(d1=(2,)),
+    t0=dict(out=(2,)),
     q0=dict(q=(0,)),
-    q1=dict(u0=(3,), k=(0,)),
-    q2=dict(v=(0,)),
-    q3=dict(d0=(3,), d1=(2,), u1=(3,), out=(2,), q=(1,)),
-    z0=dict(k=(1,), v=(1,)),
-    z1=dict(d1=(3,), u0=(4,), u1=(4,), out=(3,), q=(2,), k=(2,), v=(2,)),
-    z2=dict(d0=(4,), d1=(4,), out=(4,), q=(3,), k=(3,), v=(3,)),
-    z3=dict(d0=(5,), d1=(5,), u0=(5,), u1=(5,), out=(5,), q=(4,), k=(4,), v=(4,)),
+    q1=dict(u1=(3,)),
+    q2=dict(u0=(3,), v=(0,)),
+    q3=dict(k=(0,)),
+    z0=dict(d0=(2,), q=(1,), v=(1,)),
+    z1=dict(d1=(3,), out=(3,), k=(1,)),
+    z2=dict(d0=(3,), u0=(4,), u1=(4,), q=(2,), k=(2,), v=(2, 3,)),
+    z3=dict(d0=(4,), d1=(4,), out=(4,), q=(3,), k=(3,)),
 )
 HEADS = ("q", "k", "v")
 

time: 117 us -> 101 us (0.86)
  Pallas kernels: 116 us -> 100 us
    pallas_call x1, Pallas kernels: 113 us -> 97 us  [whole(): pl.pallas_call(kernel, out_shape=[jax.ShapeDtypeStruct(shape, F32) for sh...]
where the time goes in v4:
time: 101 us
  Pallas kernels  100 us (99%)
    pallas_call x1, Pallas kernels, whole(): pl.pallas_call(kernel, out_shape=[jax.ShapeDtypeStruct(shape, F32) for sh...  97 us
    pallas_call x1, Pallas kernels, last(): pl.pallas_call(lambda *refs: last_kernel(features, *refs), out_shape=[jax...  3.32 us

profile of v4, /device:TPU:0, one launch (start us, length us, event | category | flops | bytes accessed | tf_op | source)
XLA Modules:
  0.0 101.2 jit_solution(3840858504234685526)
XLA Ops:
  0.6 97.0 %whole.1 = (f32[2048,128]{1,0:T(8,128)}, f32[2048,128]{1,0:T(8,128)}, f32[64,512]{1,0:T(8,128)}, f32[64,512]{1,0:T(8,128)}, f32[64,128]{1,0:T(8,128)}, /*index=5...) custom-call(s32[2]{0:T(128)} %refs_0_.1, f32[1,512]{1,0:T(1,128)} %bitcast.45, f32[1,512]{1,0:T(1,128)} %bitcast.46, ...), custom_call_target="tpu_custom_call" | custom-call | tf_op jit(solution)/shard_map/whole/pallas_call | solution.py:967
  97.7 3.3 %last.1 = (f32[2048,128]{1,0:T(8,128)}, f32[2048,128]{1,0:T(8,128)}, f32[64,512]{1,0:T(8,128)}, f32[64,512]{1,0:T(8,128)}, f32[64,128]{1,0:T(8,128)}, /*index=5*...) custom-call(f32[8,16,128]{2,1,0:T(8,128)} %bitcast.43, ...), custom_call_target="tpu_custom_call" | custom-call | tf_op jit(solution)/shard_map/last/pallas_call | solution.py:994
